TPU v7x, 32 devices: a whole 2x2x4 slice. The times are simulated.
32 devices in a mesh: batch: 2 (over x), ysp: 4 (over z), xsp: 4 (over y, core).
Axes of the slice: x: 2, y: 2, z: 4, core: 2. Of those that a mesh axis runs over, the one named last changes fastest.
Arguments:
- volume: bfloat16 [640, 96, 96, 64], P('batch', 'xsp', 'ysp'), parts along dimension 0
- filter_taps: float32 [3, 3, 15], replicated
- mix_weights: bfloat16 [3, 320, 320], replicated
- mix_bias: float32 [3, 320], replicated
Outputs:
- output: bfloat16 [640, 96, 96, 64], P('batch', 'xsp', 'ysp'), parts along dimension 0
There are 2 independent parts. A program takes and returns all parts, laid end to end along the dimension named above; an argument that names none is the same for every part.
All inputs are finite; a program needn't handle non-finite values.
Results may differ from a plain program's by a relative error of at most 0.00554118.
Values are sent between devices in bfloat16 or wider.
A program may use at most 1 GiB of HBM per device.

v0:
```python
import functools

import jax
import jax.numpy as jnp
from jax import lax
from jax.experimental import pallas as pl
from jax.experimental.pallas import tpu as pltpu
from jax.sharding import PartitionSpec as P


PARTS_AXIS = "batch"
COL_AXIS = "ysp"
ROW_AXIS = "xsp"
BF = jnp.bfloat16
F32 = jnp.float32
ZB = 16
VMEM_BYTES = 67043328


class Dims:
    def __init__(self, shape, taps):
        self.c, self.nx, self.ny, self.nz = shape
        self.h = (taps - 1) // 2
        self.taps = taps
        self.cm = 256
        self.cr = self.c - self.cm
        self.rep = self.cm // self.cr
        self.rows = self.nz + self.nz // self.rep
        self.slabs = self.rows // ZB
        self.mid = self.nx - 2 * self.h


def params(nbytes):
    return dict(
        cost_estimate=pl.CostEstimate(flops=0, bytes_accessed=int(nbytes), transcendentals=0),
        compiler_params=pltpu.CompilerParams(vmem_limit_bytes=VMEM_BYTES),
    )


def banded(d, taps_ref, row, out_of, in_of, n_out):
    shape = (n_out * ZB, (2 * d.h + d.mid) * ZB)
    r = lax.broadcasted_iota(jnp.int32, shape, 0)
    s = lax.broadcasted_iota(jnp.int32, shape, 1)
    diff = jnp.where((r & (ZB - 1)) == (s & (ZB - 1)), in_of(s // ZB) - out_of(r // ZB) + d.h, -1)
    acc = jnp.zeros(shape, F32)
    for t in range(d.taps):
        acc = jnp.where(diff == t, taps_ref[row, t], acc)
    return acc.astype(BF)


def build_kernel(d, taps_ref, inner_ref, mid_ref, outer_ref, y_ref, z_ref):
    h, mid, n = d.h, d.mid, d.nx
    for layer in range(z_ref.shape[0]):
        fx, fy, fz = 3 * layer, 3 * layer + 1, 3 * layer + 2
        inner_ref[layer] = banded(d, taps_ref, fx, lambda m: h + mid + m, lambda p: jnp.where(p < mid + h, h + p, 2 * n - 1 - p), h)
        mid_ref[layer] = banded(d, taps_ref, fx, lambda m: h + m, lambda p: p, mid)
        outer_ref[layer] = banded(d, taps_ref, fx, lambda m: m, lambda p: jnp.where(p < h, -1 - p, p - h), h)
        y_ref[layer] = banded(d, taps_ref, fy, lambda m: h + m, lambda p: p, mid)
        zr = lax.broadcasted_iota(jnp.int32, (d.nz, d.nz), 0)
        zs = lax.broadcasted_iota(jnp.int32, (d.nz, d.nz), 1)
        acc = jnp.zeros((d.nz, d.nz), F32)
        for t in range(d.taps):
            acc = jnp.where(zs - zr + d.h == t, taps_ref[fz, t], acc)
        z_ref[layer] = acc.astype(BF)


def build_bands(d, taps):
    n_layers = taps.shape[0]
    cols = (2 * d.h + d.mid) * ZB
    shapes = [(d.h * ZB, cols), (d.mid * ZB, cols), (d.h * ZB, cols), (d.mid * ZB, cols), (d.nz, d.nz)]
    return pl.pallas_call(
        functools.partial(build_kernel, d),
        out_shape=[jax.ShapeDtypeStruct((n_layers,) + s, BF) for s in shapes],
        in_specs=[pl.BlockSpec(memory_space=pltpu.SMEM)],
        out_specs=[pl.BlockSpec(memory_space=pltpu.VMEM)] * len(shapes),
        name="bands",
        **params(1e6),
    )(taps.reshape(n_layers * 3, d.taps))


def lane_block(d, n_rows):
    return lax.broadcasted_iota(jnp.int32, (n_rows, d.cm), 1) // d.cr


def pack_rest(d, spread):
    step = d.nz // d.rep
    blk = lane_block(d, step)
    out = spread[0:step]
    for q in range(1, d.rep):
        out = jnp.where(blk == q, spread[q * step:(q + 1) * step], out)
    return out


def pack_kernel(d, flip_ref, v_ref, dep_ref, o_ref):
    m = lax.broadcasted_iota(jnp.int32, (d.cr, d.cm), 0)
    n = lax.broadcasted_iota(jnp.int32, (d.cr, d.cm), 1)
    spread_mat = jnp.where(n % d.cr == m, 1.0, 0.0).astype(BF)
    for y in range(d.ny):
        o_ref[0, y, 0:d.nz, :] = v_ref[0, y, :, 0:d.cm]
        rest = v_ref[0, y, :, d.cm:d.c]
        spread = jnp.dot(rest, spread_mat, preferred_element_type=F32)
        o_ref[0, y, d.nz:d.rows, :] = pack_rest(d, spread).astype(BF)


def mirrored(d, u, flip):
    return u + flip * (d.nx - 1 - 2 * u)


def pack(d, dep, flip, vol, u0, n):
    return pl.pallas_call(
        functools.partial(pack_kernel, d),
        out_shape=jax.ShapeDtypeStruct((n, d.ny, d.rows, d.cm), BF),
        grid_spec=pltpu.PrefetchScalarGridSpec(
            num_scalar_prefetch=1,
            grid=(n,),
            in_specs=[
                pl.BlockSpec((1, d.ny, d.nz, d.c), lambda i, f: (mirrored(d, u0 + i, f[0]), 0, 0, 0)),
                pl.BlockSpec(memory_space=pl.ANY),
            ],
            out_specs=pl.BlockSpec((1, d.ny, d.rows, d.cm), lambda i, f: (i, 0, 0, 0)),
        ),
        name="pack",
        **params(n * 2.2e6),
    )(flip, vol, dep)


def xfilt_kernel(d, jobs, n_ins, n_mats, *refs):
    mats = [r[...] for r in refs[:n_mats]]
    ins = refs[n_mats:n_mats + n_ins]
    outs = refs[n_mats + n_ins + 1:]
    for out, (mat, planes) in zip(outs, jobs):
        n_out = out.shape[0]
        for s in range(d.slabs):
            sl = slice(s * ZB, (s + 1) * ZB)
            rhs = jnp.concatenate([ins[p][:, 0, sl, :].reshape(ins[p].shape[0] * ZB, d.cm) for p in planes], axis=0)
            res = jnp.dot(mats[mat], rhs, preferred_element_type=F32)
            out[:, 0, sl, :] = res.astype(BF).reshape(n_out, ZB, d.cm)


def xfilt(d, dep, mats, ins, jobs, steps):
    in_specs = [pl.BlockSpec(m.shape, lambda i: (0, 0)) for m in mats]
    for a, y_of in ins:
        in_specs.append(pl.BlockSpec((a.shape[0], 1, d.rows, d.cm), lambda i, f=y_of: (0, f(i), 0, 0)))
    in_specs.append(pl.BlockSpec(memory_space=pl.ANY))
    n_outs = [mats[m].shape[0] // ZB for m, _ in jobs]
    moved = sum(a.shape[0] for a, _ in ins) + sum(n_outs)
    return pl.pallas_call(
        functools.partial(xfilt_kernel, d, jobs, len(ins), len(mats)),
        grid=(steps,),
        out_shape=[jax.ShapeDtypeStruct((n, steps, d.rows, d.cm), BF) for n in n_outs],
        in_specs=in_specs,
        out_specs=[pl.BlockSpec((n, 1, d.rows, d.cm), lambda i: (0, i, 0, 0)) for n in n_outs],
        name="xfilt",
        **params(steps * moved * 40960),
    )(*mats, *[a for a, _ in ins], dep)


def xfilt_edges(d, dep, mat, trio):
    ins = [(a, lambda i: i) for a in trio] + [(a, lambda i: d.h + d.mid + i) for a in trio]
    return xfilt(d, dep, [mat], ins, [(0, (0, 1, 2)), (0, (3, 4, 5))], d.h)


def gelu(x):
    return x * (0.5 * (1.0 + jnp.tanh(0.7978845608028654 * (x + 0.044715 * (x * x * x)))))


def tail_kernel(d, last, flip_ref, t_ref, z_ref, wm_ref, wr_ref, b_ref, hl, lo, mi, hi, hr, v_ref, dep_ref, *rest_refs):
    o_ref, um_ref, ur_ref = rest_refs[-3:]
    h, step = d.h, d.nz // d.rep
    parts = (
        (0, h, slice(0, h * ZB), (hl, lo, mi)),
        (h, d.mid, slice(0, d.mid * ZB), (lo, mi, hi)),
        (h + d.mid, h, slice((d.mid - h) * ZB, d.mid * ZB), (mi, hi, hr)),
    )
    z_mat = z_ref[...]
    b_main = b_ref[0:1, :]
    b_rest = b_ref[1:2, :]
    for y0, n, rows, trio in parts:
        t_mat = t_ref[rows, :]
        for s in range(d.slabs):
            sl = slice(s * ZB, (s + 1) * ZB)
            rhs = jnp.concatenate([r[0, :, sl, :].reshape(r.shape[1] * ZB, d.cm) for r in trio], axis=0)
            res = jnp.dot(t_mat, rhs, preferred_element_type=F32)
            if s * ZB < d.nz:
                um_ref[y0:y0 + n, sl, :] = res.astype(BF).reshape(n, ZB, d.cm)
            else:
                r0 = s * ZB - d.nz
                for q in range(d.rep):
                    piece = res[:, q * d.cr:(q + 1) * d.cr].astype(BF).reshape(n, ZB, d.cr)
                    ur_ref[y0:y0 + n, q * step + r0:q * step + r0 + ZB, :] = piece
    mains, rests = [], []
    for y in range(d.ny):
        mains.append(jnp.dot(z_mat, um_ref[y], preferred_element_type=F32).astype(BF))
        rests.append(jnp.dot(z_mat, ur_ref[y], preferred_element_type=F32).astype(BF))
    um = jnp.concatenate(mains, axis=0)
    ur = jnp.concatenate(rests, axis=0)
    main = jnp.dot(um, wm_ref[:, 0:d.cm], preferred_element_type=F32) + jnp.dot(ur, wr_ref[:, 0:d.cm], preferred_element_type=F32)
    rest = jnp.dot(um, wm_ref[:, d.cm:], preferred_element_type=F32) + jnp.dot(ur, wr_ref[:, d.cm:], preferred_element_type=F32)
    for y in range(d.ny):
        m = gelu(main[y * d.nz:(y + 1) * d.nz] + b_main) + v_ref[0, y, 0:d.nz, :].astype(F32)
        r = gelu(pack_rest(d, rest[y * d.nz:(y + 1) * d.nz]) + b_rest) + v_ref[0, y, d.nz:d.rows, :].astype(F32)
        if last:
            o_ref[0, y, :, 0:d.cm] = m.astype(BF)
            for q in range(d.rep):
                o_ref[0, y, q * step:(q + 1) * step, d.cm:d.c] = r[:, q * d.cr:(q + 1) * d.cr].astype(BF)
        else:
            o_ref[0, y, 0:d.nz, :] = m.astype(BF)
            o_ref[0, y, d.nz:d.rows, :] = r.astype(BF)


def tail(d, dep, flip, consts, us, v, last=False, u0=0, out_buf=None):
    n = v.shape[0]
    in_specs = [pl.BlockSpec(a.shape, lambda i, f: (0, 0)) for a in consts]
    for a in list(us) + [v]:
        in_specs.append(pl.BlockSpec((1,) + a.shape[1:], lambda i, f: (i, 0, 0, 0)))
    args = [flip] + list(consts) + list(us) + [v, dep]
    in_specs.append(pl.BlockSpec(memory_space=pl.ANY))
    alias = {}
    if last:
        out_shape = jax.ShapeDtypeStruct((d.nx, d.ny, d.nz, d.c), BF)
        out_spec = pl.BlockSpec((1, d.ny, d.nz, d.c), lambda i, f: (mirrored(d, u0 + i, f[0]), 0, 0, 0))
        if out_buf is not None:
            alias = {len(args): 0}
            args.append(out_buf)
            in_specs.append(pl.BlockSpec(memory_space=pl.ANY))
    else:
        out_shape = jax.ShapeDtypeStruct((n, d.ny, d.rows, d.cm), BF)
        out_spec = pl.BlockSpec((1, d.ny, d.rows, d.cm), lambda i, f: (i, 0, 0, 0))
    return pl.pallas_call(
        functools.partial(tail_kernel, d, last),
        out_shape=out_shape,
        grid_spec=pltpu.PrefetchScalarGridSpec(
            num_scalar_prefetch=1,
            grid=(n,),
            in_specs=in_specs,
            out_specs=out_spec,
            scratch_shapes=[pltpu.VMEM((d.ny, d.nz, d.cm), BF), pltpu.VMEM((d.ny, d.nz, d.cr), BF)],
        ),
        input_output_aliases=alias,
        name="tail",
        **params(n * 3.6e6),
    )(*args)


def solution(mesh):
    x_count = mesh.shape[ROW_AXIS]
    y_count = mesh.shape[COL_AXIS]
    vol_spec = P(PARTS_AXIS, ROW_AXIS, COL_AXIS, None)

    def swap(a, first):
        pairs = [(s, s + 1) for s in range(first, x_count - 1, 2)]
        return lax.ppermute(a, ROW_AXIS, pairs + [(b, a_) for a_, b in pairs])

    def share(lo, hi):
        below = lax.ppermute(hi, COL_AXIS, [(s, s + 1) for s in range(y_count - 1)])
        above = lax.ppermute(lo, COL_AXIS, [(s + 1, s) for s in range(y_count - 1)])
        return below, above

    def local_layers(volume, filter_taps, mix_weights, mix_bias):
        n_layers = filter_taps.shape[0]
        d = Dims(volume.shape, filter_taps.shape[-1])
        h, mid = d.h, d.mid
        middle = lambda i: h + i
        odd = lax.axis_index(ROW_AXIS) % 2
        flip = odd.astype(jnp.int32).reshape(1)
        taps = filter_taps.at[:, 0].set(jnp.where(odd == 1, filter_taps[:, 0, ::-1], filter_taps[:, 0]))
        vol = jnp.transpose(volume, (1, 2, 3, 0))
        w_ext = jnp.concatenate([mix_weights[:, :, :d.cm]] + [mix_weights[:, :, d.cm:]] * d.rep, axis=2)
        bias = jnp.stack([mix_bias[:, :d.cm], jnp.concatenate([mix_bias[:, d.cm:]] * d.rep, axis=1)], axis=1)
        v_in = pack(d, flip, flip, vol, h + mid, h)
        h_in = swap(v_in, 0)
        v_out = pack(d, v_in, flip, vol, 0, h)
        h_out = swap(v_out, 1)
        v_mid = pack(d, v_out, flip, vol, h, mid)
        t_in, t_mid, t_out, t_y, t_z = build_bands(d, taps)
        lo_in, hi_in = xfilt_edges(d, v_mid, t_in[0], (v_mid, v_in, h_in))
        s_in = share(lo_in, hi_in)
        dep = lo_in
        res = None
        for layer in range(n_layers):
            last = layer == n_layers - 1
            consts = (t_y[layer], t_z[layer], w_ext[layer, :d.cm], w_ext[layer, d.cm:], bias[layer])
            if layer > 0:
                h_out = swap(v_out, 1)
            lo_mid, hi_mid = xfilt_edges(d, dep, t_mid[layer], (v_out, v_mid, v_in))
            s_mid = share(lo_mid, hi_mid)
            m_mid, m_in = xfilt(
                d, lo_mid, [t_mid[layer], t_in[layer]],
                [(a, middle) for a in (v_out, v_mid, v_in, h_in)],
                [(0, (0, 1, 2)), (1, (1, 2, 3))], mid,
            )
            w_in = tail(d, m_mid, flip, consts, (s_in[0], lo_in, m_in, hi_in, s_in[1]), v_in, last, h + mid)
            if not last:
                h_in = swap(w_in, 0)
            dep = m_mid if last else w_in
            lo_out, hi_out = xfilt_edges(d, dep, t_out[layer], (h_out, v_out, v_mid))
            s_out = share(lo_out, hi_out)
            (m_out,) = xfilt(
                d, lo_out, [t_out[layer]],
                [(a, middle) for a in (h_out, v_out, v_mid)], [(0, (0, 1, 2))], mid,
            )
            w_mid = tail(d, m_out, flip, consts, (s_mid[0], lo_mid, m_mid, hi_mid, s_mid[1]), v_mid, last, h, w_in if last else None)
            us_out = (s_out[0], lo_out, m_out, hi_out, s_out[1])
            if last:
                res = tail(d, m_out, flip, consts, us_out, v_out, last, 0, w_mid)
                break
            lo_in, hi_in = xfilt_edges(d, w_mid, t_in[layer + 1], (w_mid, w_in, h_in))
            s_in = share(lo_in, hi_in)
            w_out = tail(d, lo_in, flip, consts, us_out, v_out)
            v_in, v_mid, v_out = w_in, w_mid, w_out
            dep = w_out
        return jnp.transpose(res, (3, 0, 1, 2))

    return jax.shard_map(local_layers, mesh=mesh, in_specs=(vol_spec, P(), P(), P()), out_specs=vol_spec, check_vma=False)
```

profile of v0, /device:TPU:1, one launch (start us, length us, event | category | flops | bytes accessed | tf_op | source)
XLA Modules:
  0.0 641.0 jit_solution(11816507809581066935)
XLA Ops:
  1.3 9.6 %pack.3.dep_ref.refs_2_.refs_5_.refs_3_.refs_6_.refs_4_.v_ref = bf16[7,24,80,256]{3,2,1,0:T(8,128)(2,1)} custom-call(s32[1]{0:T(128)} %bitcast.flip_ref.dep_ref, bf16[24,24,64,320]{3,2,1,0:T(8,128)(2,1)} %bitcast.51, s32[1]{0:T(128)} %bitcast.flip_ref.dep_ref), custom_call_target="tpu_custom_call" | custom-call | bytes 15400000 | tf_op jit(solution)/shard_map/pack/pallas_call | solution.py:110
  10.9 9.6 %pack.4.dep_ref.refs_1_.refs_4_.refs_2_.refs_5_.v_ref = bf16[7,24,80,256]{3,2,1,0:T(8,128)(2,1)} custom-call(s32[1]{0:T(128)} %bitcast.flip_ref.dep_ref, bf16[24,24,64,320]{3,2,1,0:T(8,128)(2,1)} %bitcast.52, bf16[7,24,80,256]{3,2,1,0:T(8,128)(2,1)} %pack.3.dep_ref.refs_2_.refs_5_.refs_3_.refs_6_.refs_4_.v_ref), custom_call_target="tpu_custom_call" | custom-call | bytes 15400000 | tf_op jit(solution)/shard_map/pack/pallas_call | solution.py:110
  20.5 12.3 %pack.5.refs_1_.refs_4_.refs_7_.refs_2_.refs_5_.refs_3_.refs_6_.v_ref = bf16[10,24,80,256]{3,2,1,0:T(8,128)(2,1)} custom-call(s32[1]{0:T(128)} %bitcast.flip_ref.dep_ref, bf16[24,24,64,320]{3,2,1,0:T(8,128)(2,1)} %bitcast.53, bf16[7,24,80,256]{3,2,1,0:T(8,128)(2,1)} %pack.4.dep_ref.refs_1_.refs_4_.refs_2_.refs_5_.v_ref), custom_call_target="tpu_custom_call" | custom-call | bytes 22000000 | tf_op jit(solution)/shard_map/pack/pallas_call | solution.py:110
  42.9 10.1 %xfilt.15 = (bf16[7,7,80,256]{3,2,1,0:T(8,128)(2,1)}, bf16[7,7,80,256]{3,2,1,0:T(8,128)(2,1)}) custom-call(bf16[112,384]{1,0:T(8,128)(2,1)} %get-tuple-element.89.refs_0_.refs_1_, bf16[10,24,80,256]{3,2,1,0:T(8,128)(2,1)} %pack.5.refs_1_.refs_4_.refs_7_.refs_2_.refs_5_.refs_3_.refs_6_.v_ref, ...), custom_call_target="tpu_custom_call" | custom-call | bytes 17776640 | tf_op jit(solution)/shard_map/xfilt/pallas_call | solution.py:147
  72.9 11.1 %xfilt.16 = (bf16[10,7,80,256]{3,2,1,0:T(8,128)(2,1)}, bf16[10,7,80,256]{3,2,1,0:T(8,128)(2,1)}) custom-call(bf16[160,384]{1,0:T(8,128)(2,1)} %get-tuple-element.83.refs_0_, bf16[7,24,80,256]{3,2,1,0:T(8,128)(2,1)} %pack.4.dep_ref.refs_1_.refs_4_.refs_2_.refs_5_.v_ref, ...), custom_call_target="tpu_custom_call" | custom-call | bytes 19496960 | tf_op jit(solution)/shard_map/xfilt/pallas_call | solution.py:147
  84.0 12.0 %xfilt.17 = (bf16[10,10,80,256]{3,2,1,0:T(8,128)(2,1)}, bf16[7,10,80,256]{3,2,1,0:T(8,128)(2,1)}) custom-call(bf16[160,384]{1,0:T(8,128)(2,1)} %get-tuple-element.83.refs_0_, bf16[112,384]{1,0:T(8,128)(2,1)} %get-tuple-element.89.refs_0_.refs_1_, bf16[7,24,80,256]{3,2,1,0:T(8,128)(2,1)} %pack.4.dep_ref.refs_1_.refs_4_.refs_2_.refs_5_.v_ref, ...), custom_call_target="tpu_custom_call" | custom-call | bytes 19660800 | tf_op jit(solution)/shard_map/xfilt/pallas_call | solution.py:147
  106.3 19.5 %tail.9.refs_7_.refs_2_.refs_5_.refs_3_.refs_6_.refs_4_.v_ref = bf16[7,24,80,256]{3,2,1,0:T(8,128)(2,1)} custom-call(s32[1]{0:T(128)} %bitcast.flip_ref.dep_ref, bf16[160,384]{1,0:T(8,128)(2,1)} %get-tuple-element.84.t_ref, bf16[64,64]{1,0:T(8,128)(2,1)} %get-tuple-element.93.z_ref, bf16[256,512]{1,0:T(8,128)(2,1)} %get-tuple-element.78.wm_ref, ...), custom_call_target="tpu_custom_call" | custom-call | bytes 25200000 | tf_op jit(solution)/shard_map/tail/pallas_call | solution.py:229
  139.6 10.1 %xfilt.18 = (bf16[7,7,80,256]{3,2,1,0:T(8,128)(2,1)}, bf16[7,7,80,256]{3,2,1,0:T(8,128)(2,1)}) custom-call(bf16[112,384]{1,0:T(8,128)(2,1)} %get-tuple-element.90.refs_0_, bf16[7,24,80,256]{3,2,1,0:T(8,128)(2,1)} %collective-permute-done.refs_1_.refs_4_, bf16[7,24,80,256]{3,2,1,0:T(8,128)(2,1)} %pack.4.dep_ref.refs_1_.refs_4_.refs_2_.refs_5_.v_ref, ...), custom_call_target="tpu_custom_call" | custom-call | bytes 17776640 | tf_op jit(solution)/shard_map/xfilt/pallas_call | solution.py:147
  156.5 9.6 %xfilt.19.dep_ref.mi = bf16[7,10,80,256]{3,2,1,0:T(8,128)(2,1)} custom-call(bf16[112,384]{1,0:T(8,128)(2,1)} %get-tuple-element.90.refs_0_, bf16[7,24,80,256]{3,2,1,0:T(8,128)(2,1)} %collective-permute-done.refs_1_.refs_4_, bf16[7,24,80,256]{3,2,1,0:T(8,128)(2,1)} %pack.4.dep_ref.refs_1_.refs_4_.refs_2_.refs_5_.v_ref, ...), custom_call_target="tpu_custom_call" | custom-call | bytes 12697600 | tf_op jit(solution)/shard_map/xfilt/pallas_call | solution.py:147
  166.1 24.5 %collective-permute-done.6.hl = bf16[10,7,80,256]{3,2,1,0:T(8,128)(2,1)} collective-permute-done((bf16[10,7,80,256]{3,2,1,0:T(8,128)(2,1)}, bf16[10,7,80,256]{3,2,1,0:T(8,128)(2,1)}, u32[]{:S(2)}, u32[]{:S(2)}) %collective-permute-start.6) | collective-permute-done | bytes 2867232 | tf_op jit(solution)/shard_map/ppermute | solution.py:255
  195.9 26.5 %tail.10.refs_1_.refs_4_.refs_7_.refs_2_.refs_5_.refs_3_.refs_6_.v_ref = bf16[10,24,80,256]{3,2,1,0:T(8,128)(2,1)} custom-call(s32[1]{0:T(128)} %bitcast.flip_ref.dep_ref, bf16[160,384]{1,0:T(8,128)(2,1)} %get-tuple-element.84.t_ref, bf16[64,64]{1,0:T(8,128)(2,1)} %get-tuple-element.93.z_ref, bf16[256,512]{1,0:T(8,128)(2,1)} %get-tuple-element.78.wm_ref, ...), custom_call_target="tpu_custom_call" | custom-call | bytes 36000000 | tf_op jit(solution)/shard_map/tail/pallas_call | solution.py:229
  222.4 10.1 %xfilt.20 = (bf16[7,7,80,256]{3,2,1,0:T(8,128)(2,1)}, bf16[7,7,80,256]{3,2,1,0:T(8,128)(2,1)}) custom-call(bf16[112,384]{1,0:T(8,128)(2,1)} %get-tuple-element.88.refs_0_.refs_1_, bf16[10,24,80,256]{3,2,1,0:T(8,128)(2,1)} %tail.10.refs_1_.refs_4_.refs_7_.refs_2_.refs_5_.refs_3_.refs_6_.v_ref, ...), custom_call_target="tpu_custom_call" | custom-call | bytes 17776640 | tf_op jit(solution)/shard_map/xfilt/pallas_call | solution.py:147
  238.9 19.4 %tail.11.refs_1_.refs_4_.refs_7_.refs_2_.refs_5_.v_ref = bf16[7,24,80,256]{3,2,1,0:T(8,128)(2,1)} custom-call(s32[1]{0:T(128)} %bitcast.flip_ref.dep_ref, bf16[160,384]{1,0:T(8,128)(2,1)} %get-tuple-element.84.t_ref, bf16[64,64]{1,0:T(8,128)(2,1)} %get-tuple-element.93.z_ref, bf16[256,512]{1,0:T(8,128)(2,1)} %get-tuple-element.78.wm_ref, ...), custom_call_target="tpu_custom_call" | custom-call | bytes 25200000 | tf_op jit(solution)/shard_map/tail/pallas_call | solution.py:229
  262.5 11.1 %xfilt.21 = (bf16[10,7,80,256]{3,2,1,0:T(8,128)(2,1)}, bf16[10,7,80,256]{3,2,1,0:T(8,128)(2,1)}) custom-call(bf16[160,384]{1,0:T(8,128)(2,1)} %get-tuple-element.82.refs_0_, bf16[7,24,80,256]{3,2,1,0:T(8,128)(2,1)} %tail.11.refs_1_.refs_4_.refs_7_.refs_2_.refs_5_.v_ref, ...), custom_call_target="tpu_custom_call" | custom-call | bytes 19496960 | tf_op jit(solution)/shard_map/xfilt/pallas_call | solution.py:147
  273.6 12.0 %xfilt.22 = (bf16[10,10,80,256]{3,2,1,0:T(8,128)(2,1)}, bf16[7,10,80,256]{3,2,1,0:T(8,128)(2,1)}) custom-call(bf16[160,384]{1,0:T(8,128)(2,1)} %get-tuple-element.82.refs_0_, bf16[112,384]{1,0:T(8,128)(2,1)} %get-tuple-element.88.refs_0_.refs_1_, bf16[7,24,80,256]{3,2,1,0:T(8,128)(2,1)} %tail.11.refs_1_.refs_4_.refs_7_.refs_2_.refs_5_.v_ref, ...), custom_call_target="tpu_custom_call" | custom-call | bytes 19660800 | tf_op jit(solution)/shard_map/xfilt/pallas_call | solution.py:147
  285.7 19.4 %tail.12.refs_7_.refs_2_.refs_5_.refs_3_.refs_6_.refs_4_.v_ref = bf16[7,24,80,256]{3,2,1,0:T(8,128)(2,1)} custom-call(s32[1]{0:T(128)} %bitcast.flip_ref.dep_ref, bf16[160,384]{1,0:T(8,128)(2,1)} %get-tuple-element.85.t_ref, bf16[64,64]{1,0:T(8,128)(2,1)} %get-tuple-element.94.z_ref, bf16[256,512]{1,0:T(8,128)(2,1)} %get-tuple-element.79.wm_ref, ...), custom_call_target="tpu_custom_call" | custom-call | bytes 25200000 | tf_op jit(solution)/shard_map/tail/pallas_call | solution.py:229
  311.5 26.6 %collective-permute-done.9.refs_1_.refs_4_ = bf16[7,24,80,256]{3,2,1,0:T(8,128)(2,1)} collective-permute-done((bf16[7,24,80,256]{3,2,1,0:T(8,128)(2,1)}, bf16[7,24,80,256]{3,2,1,0:T(8,128)(2,1)}, u32[]{:S(2)}, u32[]{:S(2)}) %collective-permute-start.9) | collective-permute-done | bytes 6881312 | tf_op jit(solution)/shard_map/ppermute | solution.py:252
  338.1 10.1 %xfilt.23 = (bf16[7,7,80,256]{3,2,1,0:T(8,128)(2,1)}, bf16[7,7,80,256]{3,2,1,0:T(8,128)(2,1)}) custom-call(bf16[112,384]{1,0:T(8,128)(2,1)} %get-tuple-element.91.refs_0_, bf16[7,24,80,256]{3,2,1,0:T(8,128)(2,1)} %collective-permute-done.9.refs_1_.refs_4_, bf16[7,24,80,256]{3,2,1,0:T(8,128)(2,1)} %tail.11.refs_1_.refs_4_.refs_7_.refs_2_.refs_5_.v_ref, ...), custom_call_target="tpu_custom_call" | custom-call | bytes 17776640 | tf_op jit(solution)/shard_map/xfilt/pallas_call | solution.py:147
  354.2 9.6 %xfilt.24.dep_ref.mi = bf16[7,10,80,256]{3,2,1,0:T(8,128)(2,1)} custom-call(bf16[112,384]{1,0:T(8,128)(2,1)} %get-tuple-element.91.refs_0_, bf16[7,24,80,256]{3,2,1,0:T(8,128)(2,1)} %collective-permute-done.9.refs_1_.refs_4_, bf16[7,24,80,256]{3,2,1,0:T(8,128)(2,1)} %tail.11.refs_1_.refs_4_.refs_7_.refs_2_.refs_5_.v_ref, ...), custom_call_target="tpu_custom_call" | custom-call | bytes 12697600 | tf_op jit(solution)/shard_map/xfilt/pallas_call | solution.py:147
  363.8 6.5 %collective-permute-done.14.hl = bf16[10,7,80,256]{3,2,1,0:T(8,128)(2,1)} collective-permute-done((bf16[10,7,80,256]{3,2,1,0:T(8,128)(2,1)}, bf16[10,7,80,256]{3,2,1,0:T(8,128)(2,1)}, u32[]{:S(2)}, u32[]{:S(2)}) %collective-permute-start.14) | collective-permute-done | bytes 2867232 | tf_op jit(solution)/shard_map/ppermute | solution.py:255
  375.7 26.6 %tail.13.refs_1_.refs_4_.refs_7_.refs_2_.refs_5_.refs_3_.refs_6_.v_ref = bf16[10,24,80,256]{3,2,1,0:T(8,128)(2,1)} custom-call(s32[1]{0:T(128)} %bitcast.flip_ref.dep_ref, bf16[160,384]{1,0:T(8,128)(2,1)} %get-tuple-element.85.t_ref, bf16[64,64]{1,0:T(8,128)(2,1)} %get-tuple-element.94.z_ref, bf16[256,512]{1,0:T(8,128)(2,1)} %get-tuple-element.79.wm_ref, ...), custom_call_target="tpu_custom_call" | custom-call | bytes 36000000 | tf_op jit(solution)/shard_map/tail/pallas_call | solution.py:229
  402.3 10.2 %xfilt.25 = (bf16[7,7,80,256]{3,2,1,0:T(8,128)(2,1)}, bf16[7,7,80,256]{3,2,1,0:T(8,128)(2,1)}) custom-call(bf16[112,384]{1,0:T(8,128)(2,1)} %get-tuple-element.87.refs_0_.refs_1_, bf16[10,24,80,256]{3,2,1,0:T(8,128)(2,1)} %tail.13.refs_1_.refs_4_.refs_7_.refs_2_.refs_5_.refs_3_.refs_6_.v_ref, ...), custom_call_target="tpu_custom_call" | custom-call | bytes 17776640 | tf_op jit(solution)/shard_map/xfilt/pallas_call | solution.py:147
  418.7 19.4 %tail.14.refs_1_.refs_4_.refs_7_.refs_2_.refs_5_.v_ref = bf16[7,24,80,256]{3,2,1,0:T(8,128)(2,1)} custom-call(s32[1]{0:T(128)} %bitcast.flip_ref.dep_ref, bf16[160,384]{1,0:T(8,128)(2,1)} %get-tuple-element.85.t_ref, bf16[64,64]{1,0:T(8,128)(2,1)} %get-tuple-element.94.z_ref, bf16[256,512]{1,0:T(8,128)(2,1)} %get-tuple-element.79.wm_ref, ...), custom_call_target="tpu_custom_call" | custom-call | bytes 25200000 | tf_op jit(solution)/shard_map/tail/pallas_call | solution.py:229
  443.6 11.1 %xfilt.26 = (bf16[10,7,80,256]{3,2,1,0:T(8,128)(2,1)}, bf16[10,7,80,256]{3,2,1,0:T(8,128)(2,1)}) custom-call(bf16[160,384]{1,0:T(8,128)(2,1)} %get-tuple-element.81.refs_0_, bf16[7,24,80,256]{3,2,1,0:T(8,128)(2,1)} %tail.14.refs_1_.refs_4_.refs_7_.refs_2_.refs_5_.v_ref, ...), custom_call_target="tpu_custom_call" | custom-call | bytes 19496960 | tf_op jit(solution)/shard_map/xfilt/pallas_call | solution.py:147
  460.1 12.0 %xfilt.27 = (bf16[10,10,80,256]{3,2,1,0:T(8,128)(2,1)}, bf16[7,10,80,256]{3,2,1,0:T(8,128)(2,1)}) custom-call(bf16[160,384]{1,0:T(8,128)(2,1)} %get-tuple-element.81.refs_0_, bf16[112,384]{1,0:T(8,128)(2,1)} %get-tuple-element.87.refs_0_.refs_1_, bf16[7,24,80,256]{3,2,1,0:T(8,128)(2,1)} %tail.14.refs_1_.refs_4_.refs_7_.refs_2_.refs_5_.v_ref, ...), custom_call_target="tpu_custom_call" | custom-call | bytes 19660800 | tf_op jit(solution)/shard_map/xfilt/pallas_call | solution.py:147
  472.1 45.2 %collective-permute-done.17.refs_1_.refs_4_ = bf16[7,24,80,256]{3,2,1,0:T(8,128)(2,1)} collective-permute-done((bf16[7,24,80,256]{3,2,1,0:T(8,128)(2,1)}, bf16[7,24,80,256]{3,2,1,0:T(8,128)(2,1)}, u32[]{:S(2)}, u32[]{:S(2)}) %collective-permute-start.17) | collective-permute-done | bytes 6881312 | tf_op jit(solution)/shard_map/ppermute | solution.py:252
  517.3 10.1 %xfilt.28 = (bf16[7,7,80,256]{3,2,1,0:T(8,128)(2,1)}, bf16[7,7,80,256]{3,2,1,0:T(8,128)(2,1)}) custom-call(bf16[112,384]{1,0:T(8,128)(2,1)} %get-tuple-element.92.refs_0_, bf16[7,24,80,256]{3,2,1,0:T(8,128)(2,1)} %collective-permute-done.17.refs_1_.refs_4_, bf16[7,24,80,256]{3,2,1,0:T(8,128)(2,1)} %tail.14.refs_1_.refs_4_.refs_7_.refs_2_.refs_5_.v_ref, ...), custom_call_target="tpu_custom_call" | custom-call | bytes 17776640 | tf_op jit(solution)/shard_map/xfilt/pallas_call | solution.py:147
  531.5 32.9 %collective-permute-done.23.hr = bf16[7,7,80,256]{3,2,1,0:T(8,128)(2,1)} collective-permute-done((bf16[7,7,80,256]{3,2,1,0:T(8,128)(2,1)}, bf16[7,7,80,256]{3,2,1,0:T(8,128)(2,1)}, u32[]{:S(2)}, u32[]{:S(2)}) %collective-permute-start.23) | collective-permute-done | bytes 2007072 | tf_op jit(solution)/shard_map/ppermute | solution.py:256
  564.4 19.9 %tail.15.rest_refs_0_ = bf16[24,24,64,320]{3,2,1,0:T(8,128)(2,1)} custom-call(s32[1]{0:T(128)} %bitcast.flip_ref.dep_ref, bf16[160,384]{1,0:T(8,128)(2,1)} %get-tuple-element.86.t_ref, bf16[64,64]{1,0:T(8,128)(2,1)} %get-tuple-element.95.z_ref, bf16[256,512]{1,0:T(8,128)(2,1)} %get-tuple-element.80.wm_ref, bf16[64,512]{1,0:T(8,128)(2,1)} %get-tuple-element.76.wr_ref, ...), custom_call_target="tpu_custom_call" | custom-call | bytes 25200000 | tf_op jit(solution)/shard_map/tail/pallas_call | solution.py:229
  584.3 9.6 %xfilt.29.dep_ref.mi = bf16[7,10,80,256]{3,2,1,0:T(8,128)(2,1)} custom-call(bf16[112,384]{1,0:T(8,128)(2,1)} %get-tuple-element.92.refs_0_, bf16[7,24,80,256]{3,2,1,0:T(8,128)(2,1)} %collective-permute-done.17.refs_1_.refs_4_, bf16[7,24,80,256]{3,2,1,0:T(8,128)(2,1)} %tail.14.refs_1_.refs_4_.refs_7_.refs_2_.refs_5_.v_ref, ...), custom_call_target="tpu_custom_call" | custom-call | bytes 12697600 | tf_op jit(solution)/shard_map/xfilt/pallas_call | solution.py:147
  593.9 27.2 %tail.16.rest_refs_0_ = bf16[24,24,64,320]{3,2,1,0:T(8,128)(2,1)} custom-call(s32[1]{0:T(128)} %bitcast.flip_ref.dep_ref, bf16[160,384]{1,0:T(8,128)(2,1)} %get-tuple-element.86.t_ref, bf16[64,64]{1,0:T(8,128)(2,1)} %get-tuple-element.95.z_ref, bf16[256,512]{1,0:T(8,128)(2,1)} %get-tuple-element.80.wm_ref, ...), custom_call_target="tpu_custom_call", output_to_operand_aliasing={{}: (13, {})} | custom-call | bytes 36000000 | tf_op jit(solution)/shard_map/tail/pallas_call | solution.py:229
  621.1 19.9 %tail.17 = bf16[24,24,64,320]{3,2,1,0:T(8,128)(2,1)} custom-call(s32[1]{0:T(128)} %bitcast.flip_ref.dep_ref, bf16[160,384]{1,0:T(8,128)(2,1)} %get-tuple-element.86.t_ref, bf16[64,64]{1,0:T(8,128)(2,1)} %get-tuple-element.95.z_ref, bf16[256,512]{1,0:T(8,128)(2,1)} %get-tuple-element.80.wm_ref, ...), custom_call_target="tpu_custom_call", output_to_operand_aliasing={{}: (13, {})} | custom-call | bytes 25200000 | tf_op jit(solution)/shard_map/tail/pallas_call | solution.py:229
  (71 shorter events, 117.0 us)
Async XLA Ops:
  10.9 32.0 %collective-permute-start.1 = (bf16[7,24,80,256]{3,2,1,0:T(8,128)(2,1)}, bf16[7,24,80,256]{3,2,1,0:T(8,128)(2,1)}, u32[]{:S(2)}, u32[]{:S(2)}) collective-permute-start(bf16[7,24,80,256]{3,2,1,0:T(8,128)(2,1)} %pack.3.dep_ref.refs_2_.refs_5_.refs_3_.refs_6_.refs_4_.v_ref), channel_id=1, source_target_pairs={{0,1},{2,3},{1,0},{3,2},{4,5},{6,7},{5,4},{7,6},{8,9},{10,11},{9,8... | collective-permute-start | bytes 20643848 | tf_op jit(solution)/shard_map/ppermute | solution.py:252
  53.0 16.9 %copy-start.2 = (bf16[3,64,64]{2,1,0:T(8,128)(2,1)S(1)}, bf16[3,64,64]{2,1,0:T(8,128)(2,1)}, u32[]{:S(2)}) copy-start(bf16[3,64,64]{2,1,0:T(8,128)(2,1)} %get-tuple-element.47) | copy-start | bytes 73732
  53.0 17.5 %copy-start.1 = (bf16[3,160,384]{2,1,0:T(8,128)(2,1)S(1)}, bf16[3,160,384]{2,1,0:T(8,128)(2,1)}, u32[]{:S(2)}) copy-start(bf16[3,160,384]{2,1,0:T(8,128)(2,1)} %get-tuple-element.52) | copy-start | bytes 1105924
  53.0 18.2 %copy-start = (bf16[3,160,384]{2,1,0:T(8,128)(2,1)S(1)}, bf16[3,160,384]{2,1,0:T(8,128)(2,1)}, u32[]{:S(2)}) copy-start(bf16[3,160,384]{2,1,0:T(8,128)(2,1)} %get-tuple-element.46) | copy-start | bytes 1105924
  53.0 48.1 %collective-permute-start.2 = (bf16[7,7,80,256]{3,2,1,0:T(8,128)(2,1)}, bf16[7,7,80,256]{3,2,1,0:T(8,128)(2,1)}, u32[]{:S(2)}, u32[]{:S(2)}) collective-permute-start(bf16[7,7,80,256]{3,2,1,0:T(8,128)(2,1)} %get-tuple-element.50.hi), channel_id=1, source_target_pairs={{0,4},{4,8},{8,12},{1,5},{5,9},{9,13},{2,6},{6,10},{10,14},{3,7},{... | collective-permute-start | bytes 6021128 | tf_op jit(solution)/shard_map/ppermute | solution.py:255
  59.1 47.1 %collective-permute-start.3 = (bf16[7,7,80,256]{3,2,1,0:T(8,128)(2,1)}, bf16[7,7,80,256]{3,2,1,0:T(8,128)(2,1)}, u32[]{:S(2)}, u32[]{:S(2)}) collective-permute-start(bf16[7,7,80,256]{3,2,1,0:T(8,128)(2,1)} %get-tuple-element.51.refs_7_.lo), channel_id=1, source_target_pairs={{4,0},{8,4},{12,8},{5,1},{9,5},{13,9},{6,2},{10,6},{14,10},{7,3},{... | collective-permute-start | bytes 6021128 | tf_op jit(solution)/shard_map/ppermute | solution.py:256
  60.4 79.2 %collective-permute-start = (bf16[7,24,80,256]{3,2,1,0:T(8,128)(2,1)}, bf16[7,24,80,256]{3,2,1,0:T(8,128)(2,1)}, u32[]{:S(2)}, u32[]{:S(2)}) collective-permute-start(bf16[7,24,80,256]{3,2,1,0:T(8,128)(2,1)} %pack.4.dep_ref.refs_1_.refs_4_.refs_2_.refs_5_.v_ref), channel_id=1, source_target_pairs={{1,2},{2,1},{5,6},{6,5},{9,10},{10,9},{13,14},{14,13},{17,18},{18,... | collective-permute-start | bytes 20643848 | tf_op jit(solution)/shard_map/ppermute | solution.py:252
  125.8 96.6 %collective-permute-start.8 = (bf16[7,24,80,256]{3,2,1,0:T(8,128)(2,1)}, bf16[7,24,80,256]{3,2,1,0:T(8,128)(2,1)}, u32[]{:S(2)}, u32[]{:S(2)}) collective-permute-start(bf16[7,24,80,256]{3,2,1,0:T(8,128)(2,1)} %tail.9.refs_7_.refs_2_.refs_5_.refs_3_.refs_6_.refs_4_.v_ref), channel_id=1, source_target_pairs={{0,1},{2,3},{1,0},{3,2},{4,5},{6,7},{5,4},{7,6},{8,9},{10,11},{9,8... | collective-permute-start | bytes 20643848 | tf_op jit(solution)/shard_map/ppermute | solution.py:252
  126.9 63.7 %collective-permute-start.6 = (bf16[10,7,80,256]{3,2,1,0:T(8,128)(2,1)}, bf16[10,7,80,256]{3,2,1,0:T(8,128)(2,1)}, u32[]{:S(2)}, u32[]{:S(2)}) collective-permute-start(bf16[10,7,80,256]{3,2,1,0:T(8,128)(2,1)} %get-tuple-element.58.hi), channel_id=1, source_target_pairs={{0,4},{4,8},{8,12},{1,5},{5,9},{9,13},{2,6},{6,10},{10,14},{3,7},{... | collective-permute-start | bytes 8601608 | tf_op jit(solution)/shard_map/ppermute | solution.py:255
  130.3 65.6 %collective-permute-start.7 = (bf16[10,7,80,256]{3,2,1,0:T(8,128)(2,1)}, bf16[10,7,80,256]{3,2,1,0:T(8,128)(2,1)}, u32[]{:S(2)}, u32[]{:S(2)}) collective-permute-start(bf16[10,7,80,256]{3,2,1,0:T(8,128)(2,1)} %get-tuple-element.53.refs_6_.lo), channel_id=1, source_target_pairs={{4,0},{8,4},{12,8},{5,1},{9,5},{13,9},{6,2},{10,6},{14,10},{7,3},{... | collective-permute-start | bytes 8601608 | tf_op jit(solution)/shard_map/ppermute | solution.py:256
  149.7 87.1 %collective-permute-start.4 = (bf16[7,7,80,256]{3,2,1,0:T(8,128)(2,1)}, bf16[7,7,80,256]{3,2,1,0:T(8,128)(2,1)}, u32[]{:S(2)}, u32[]{:S(2)}) collective-permute-start(bf16[7,7,80,256]{3,2,1,0:T(8,128)(2,1)} %get-tuple-element.56.hi), channel_id=1, source_target_pairs={{0,4},{4,8},{8,12},{1,5},{5,9},{9,13},{2,6},{6,10},{10,14},{3,7},{... | collective-permute-start | bytes 6021128 | tf_op jit(solution)/shard_map/ppermute | solution.py:255
  155.0 83.9 %collective-permute-start.5 = (bf16[7,7,80,256]{3,2,1,0:T(8,128)(2,1)}, bf16[7,7,80,256]{3,2,1,0:T(8,128)(2,1)}, u32[]{:S(2)}, u32[]{:S(2)}) collective-permute-start(bf16[7,7,80,256]{3,2,1,0:T(8,128)(2,1)} %get-tuple-element.57.refs_4_.lo), channel_id=1, source_target_pairs={{4,0},{8,4},{12,8},{5,1},{9,5},{13,9},{6,2},{10,6},{14,10},{7,3},{... | collective-permute-start | bytes 6021128 | tf_op jit(solution)/shard_map/ppermute | solution.py:256
  232.5 53.1 %collective-permute-start.10 = (bf16[7,7,80,256]{3,2,1,0:T(8,128)(2,1)}, bf16[7,7,80,256]{3,2,1,0:T(8,128)(2,1)}, u32[]{:S(2)}, u32[]{:S(2)}) collective-permute-start(bf16[7,7,80,256]{3,2,1,0:T(8,128)(2,1)} %get-tuple-element.60.hi), channel_id=1, source_target_pairs={{0,4},{4,8},{8,12},{1,5},{5,9},{9,13},{2,6},{6,10},{10,14},{3,7},{... | collective-permute-start | bytes 6021128 | tf_op jit(solution)/shard_map/ppermute | solution.py:255
  235.5 50.1 %collective-permute-start.11 = (bf16[7,7,80,256]{3,2,1,0:T(8,128)(2,1)}, bf16[7,7,80,256]{3,2,1,0:T(8,128)(2,1)}, u32[]{:S(2)}, u32[]{:S(2)}) collective-permute-start(bf16[7,7,80,256]{3,2,1,0:T(8,128)(2,1)} %get-tuple-element.59.dep_ref.lo), channel_id=1, source_target_pairs={{4,0},{8,4},{12,8},{5,1},{9,5},{13,9},{6,2},{10,6},{14,10},{7,3},{... | collective-permute-start | bytes 6021128 | tf_op jit(solution)/shard_map/ppermute | solution.py:256
  258.4 79.7 %collective-permute-start.9 = (bf16[7,24,80,256]{3,2,1,0:T(8,128)(2,1)}, bf16[7,24,80,256]{3,2,1,0:T(8,128)(2,1)}, u32[]{:S(2)}, u32[]{:S(2)}) collective-permute-start(bf16[7,24,80,256]{3,2,1,0:T(8,128)(2,1)} %tail.11.refs_1_.refs_4_.refs_7_.refs_2_.refs_5_.v_ref), channel_id=1, source_target_pairs={{1,2},{2,1},{5,6},{6,5},{9,10},{10,9},{13,14},{14,13},{17,18},{18,... | collective-permute-start | bytes 20643848 | tf_op jit(solution)/shard_map/ppermute | solution.py:252
  305.1 97.2 %collective-permute-start.16 = (bf16[7,24,80,256]{3,2,1,0:T(8,128)(2,1)}, bf16[7,24,80,256]{3,2,1,0:T(8,128)(2,1)}, u32[]{:S(2)}, u32[]{:S(2)}) collective-permute-start(bf16[7,24,80,256]{3,2,1,0:T(8,128)(2,1)} %tail.12.refs_7_.refs_2_.refs_5_.refs_3_.refs_6_.refs_4_.v_ref), channel_id=1, source_target_pairs={{0,1},{2,3},{1,0},{3,2},{4,5},{6,7},{5,4},{7,6},{8,9},{10,11},{9,8... | collective-permute-start | bytes 20643848 | tf_op jit(solution)/shard_map/ppermute | solution.py:252
  305.5 64.9 %collective-permute-start.14 = (bf16[10,7,80,256]{3,2,1,0:T(8,128)(2,1)}, bf16[10,7,80,256]{3,2,1,0:T(8,128)(2,1)}, u32[]{:S(2)}, u32[]{:S(2)}) collective-permute-start(bf16[10,7,80,256]{3,2,1,0:T(8,128)(2,1)} %get-tuple-element.66.hi), channel_id=1, source_target_pairs={{0,4},{4,8},{8,12},{1,5},{5,9},{9,13},{2,6},{6,10},{10,14},{3,7},{... | collective-permute-start | bytes 8601608 | tf_op jit(solution)/shard_map/ppermute | solution.py:255
  310.2 65.5 %collective-permute-start.15 = (bf16[10,7,80,256]{3,2,1,0:T(8,128)(2,1)}, bf16[10,7,80,256]{3,2,1,0:T(8,128)(2,1)}, u32[]{:S(2)}, u32[]{:S(2)}) collective-permute-start(bf16[10,7,80,256]{3,2,1,0:T(8,128)(2,1)} %get-tuple-element.61.refs_6_.lo), channel_id=1, source_target_pairs={{4,0},{8,4},{12,8},{5,1},{9,5},{13,9},{6,2},{10,6},{14,10},{7,3},{... | collective-permute-start | bytes 8601608 | tf_op jit(solution)/shard_map/ppermute | solution.py:256
  348.2 65.1 %collective-permute-start.12 = (bf16[7,7,80,256]{3,2,1,0:T(8,128)(2,1)}, bf16[7,7,80,256]{3,2,1,0:T(8,128)(2,1)}, u32[]{:S(2)}, u32[]{:S(2)}) collective-permute-start(bf16[7,7,80,256]{3,2,1,0:T(8,128)(2,1)} %get-tuple-element.64.hi), channel_id=1, source_target_pairs={{0,4},{4,8},{8,12},{1,5},{5,9},{9,13},{2,6},{6,10},{10,14},{3,7},{... | collective-permute-start | bytes 6021128 | tf_op jit(solution)/shard_map/ppermute | solution.py:255
  352.7 66.0 %collective-permute-start.13 = (bf16[7,7,80,256]{3,2,1,0:T(8,128)(2,1)}, bf16[7,7,80,256]{3,2,1,0:T(8,128)(2,1)}, u32[]{:S(2)}, u32[]{:S(2)}) collective-permute-start(bf16[7,7,80,256]{3,2,1,0:T(8,128)(2,1)} %get-tuple-element.65.refs_4_.lo), channel_id=1, source_target_pairs={{4,0},{8,4},{12,8},{5,1},{9,5},{13,9},{6,2},{10,6},{14,10},{7,3},{... | collective-permute-start | bytes 6021128 | tf_op jit(solution)/shard_map/ppermute | solution.py:256
  438.1 79.2 %collective-permute-start.17 = (bf16[7,24,80,256]{3,2,1,0:T(8,128)(2,1)}, bf16[7,24,80,256]{3,2,1,0:T(8,128)(2,1)}, u32[]{:S(2)}, u32[]{:S(2)}) collective-permute-start(bf16[7,24,80,256]{3,2,1,0:T(8,128)(2,1)} %tail.14.refs_1_.refs_4_.refs_7_.refs_2_.refs_5_.v_ref), channel_id=1, source_target_pairs={{1,2},{2,1},{5,6},{6,5},{9,10},{10,9},{13,14},{14,13},{17,18},{18,... | collective-permute-start | bytes 20643848 | tf_op jit(solution)/shard_map/ppermute | solution.py:252
  440.9 89.1 %collective-permute-start.22 = (bf16[7,7,80,256]{3,2,1,0:T(8,128)(2,1)}, bf16[7,7,80,256]{3,2,1,0:T(8,128)(2,1)}, u32[]{:S(2)}, u32[]{:S(2)}) collective-permute-start(bf16[7,7,80,256]{3,2,1,0:T(8,128)(2,1)} %get-tuple-element.73.hi), channel_id=1, source_target_pairs={{0,4},{4,8},{8,12},{1,5},{5,9},{9,13},{2,6},{6,10},{10,14},{3,7},{... | collective-permute-start | bytes 6021128 | tf_op jit(solution)/shard_map/ppermute | solution.py:255
  454.6 139.3 %collective-permute-start.20 = (bf16[10,7,80,256]{3,2,1,0:T(8,128)(2,1)}, bf16[10,7,80,256]{3,2,1,0:T(8,128)(2,1)}, u32[]{:S(2)}, u32[]{:S(2)}) collective-permute-start(bf16[10,7,80,256]{3,2,1,0:T(8,128)(2,1)} %get-tuple-element.72.hi), channel_id=1, source_target_pairs={{0,4},{4,8},{8,12},{1,5},{5,9},{9,13},{2,6},{6,10},{10,14},{3,7},{... | collective-permute-start | bytes 8601608 | tf_op jit(solution)/shard_map/ppermute | solution.py:255
  457.5 136.4 %collective-permute-start.21 = (bf16[10,7,80,256]{3,2,1,0:T(8,128)(2,1)}, bf16[10,7,80,256]{3,2,1,0:T(8,128)(2,1)}, u32[]{:S(2)}, u32[]{:S(2)}) collective-permute-start(bf16[10,7,80,256]{3,2,1,0:T(8,128)(2,1)} %get-tuple-element.68.refs_6_.lo), channel_id=1, source_target_pairs={{4,0},{8,4},{12,8},{5,1},{9,5},{13,9},{6,2},{10,6},{14,10},{7,3},{... | collective-permute-start | bytes 8601608 | tf_op jit(solution)/shard_map/ppermute | solution.py:256
  458.8 105.6 %collective-permute-start.23 = (bf16[7,7,80,256]{3,2,1,0:T(8,128)(2,1)}, bf16[7,7,80,256]{3,2,1,0:T(8,128)(2,1)}, u32[]{:S(2)}, u32[]{:S(2)}) collective-permute-start(bf16[7,7,80,256]{3,2,1,0:T(8,128)(2,1)} %get-tuple-element.67.dep_ref.lo), channel_id=1, source_target_pairs={{4,0},{8,4},{12,8},{5,1},{9,5},{13,9},{6,2},{10,6},{14,10},{7,3},{... | collective-permute-start | bytes 6021128 | tf_op jit(solution)/shard_map/ppermute | solution.py:256
  527.4 93.7 %collective-permute-start.18 = (bf16[7,7,80,256]{3,2,1,0:T(8,128)(2,1)}, bf16[7,7,80,256]{3,2,1,0:T(8,128)(2,1)}, u32[]{:S(2)}, u32[]{:S(2)}) collective-permute-start(bf16[7,7,80,256]{3,2,1,0:T(8,128)(2,1)} %get-tuple-element.70.hi), channel_id=1, source_target_pairs={{0,4},{4,8},{8,12},{1,5},{5,9},{9,13},{2,6},{6,10},{10,14},{3,7},{... | collective-permute-start | bytes 6021128 | tf_op jit(solution)/shard_map/ppermute | solution.py:255
  530.0 91.1 %collective-permute-start.19 = (bf16[7,7,80,256]{3,2,1,0:T(8,128)(2,1)}, bf16[7,7,80,256]{3,2,1,0:T(8,128)(2,1)}, u32[]{:S(2)}, u32[]{:S(2)}) collective-permute-start(bf16[7,7,80,256]{3,2,1,0:T(8,128)(2,1)} %get-tuple-element.71.refs_4_.lo), channel_id=1, source_target_pairs={{4,0},{8,4},{12,8},{5,1},{9,5},{13,9},{6,2},{10,6},{14,10},{7,3},{... | collective-permute-start | bytes 6021128 | tf_op jit(solution)/shard_map/ppermute | solution.py:256
where the time goes:
time: 651 us; the launch traced here: 641 us
  Pallas kernels  392 us (60%)
  waiting for transfers between devices  171 us (26%)
  starting transfers between devices  59.2 us (9%)
  local copies, waits for them, and re-layouts  13.4 us (2%)
    pallas_call x9, Pallas kernels, tail(): pl.pallas_call(functools.partial(tail_kernel, d, last), out_shape=out_sha...  198 us
    pallas_call x15, Pallas kernels, xfilt(): pl.pallas_call(functools.partial(xfilt_kernel, d, jobs, len(ins), len(mat...  159 us
    ppermute x6, waiting for transfers between devices, swap(): return lax.ppermute(a, ROW_AXIS, pairs + [(b, a_) for a_, b in pairs])  78.2 us
    ppermute x9, waiting for transfers between devices, share(): above = lax.ppermute(lo, COL_AXIS, [(s + 1, s) for s in range(y_count - 1)])  56.1 us
    ppermute x9, waiting for transfers between devices, share(): below = lax.ppermute(hi, COL_AXIS, [(s, s + 1) for s in range(y_count - 1)])  37 us
    ppermute x9, starting transfers between devices, share(): below = lax.ppermute(hi, COL_AXIS, [(s, s + 1) for s in range(y_count - 1)])  35.2 us
    pallas_call x3, Pallas kernels, pack(): pl.pallas_call(functools.partial(pack_kernel, d), out_shape=jax.ShapeDtyp...  31.6 us
  transfers between devices with their start and end apart: 24, of which 13 were waited for; matrix products, arithmetic and copies ran while one was open for 3% of the time, Pallas kernels for 52%

commit v1 on v0

v1 whole, which is shorter than its diff:
```python
import functools

import jax
import jax.numpy as jnp
from jax import lax
from jax.experimental import pallas as pl
from jax.experimental.pallas import tpu as pltpu
from jax.sharding import PartitionSpec as P


PARTS_AXIS = "batch"
COL_AXIS = "ysp"
ROW_AXIS = "xsp"
BF = jnp.bfloat16
F32 = jnp.float32
ZB = 16
VMEM_BYTES = 67043328


class Dims:
    def __init__(self, shape, taps):
        self.c, self.nx, self.ny, self.nz = shape
        self.h = (taps - 1) // 2
        self.taps = taps
        self.cm = 256
        self.cr = self.c - self.cm
        self.rep = self.cm // self.cr
        self.rows = self.nz + self.nz // self.rep
        self.slabs = self.rows // ZB
        self.mid = self.nx - 2 * self.h


def params(nbytes):
    return dict(
        cost_estimate=pl.CostEstimate(flops=0, bytes_accessed=int(nbytes), transcendentals=0),
        compiler_params=pltpu.CompilerParams(vmem_limit_bytes=VMEM_BYTES),
    )


def banded(d, tap_of, out_of, in_of, n_out):
    shape = (n_out * ZB, (2 * d.h + d.mid) * ZB)
    r = lax.broadcasted_iota(jnp.int32, shape, 0)
    s = lax.broadcasted_iota(jnp.int32, shape, 1)
    diff = jnp.where((r & (ZB - 1)) == (s & (ZB - 1)), in_of(s // ZB) - out_of(r // ZB) + d.h, -1)
    acc = jnp.zeros(shape, F32)
    for t in range(d.taps):
        acc = jnp.where(diff == t, tap_of(t), acc)
    return acc.astype(BF)


def x_taps(d, flip_ref, taps_ref, layer):
    flip = flip_ref[0]
    return lambda t: taps_ref[layer, 0, t + flip * (d.taps - 1 - 2 * t)]


def first_kernel(d, flip_ref, taps_ref, o_ref):
    o_ref[...] = banded(d, x_taps(d, flip_ref, taps_ref, 0), lambda m: d.h + m, lambda p: mirrored(d, p, flip_ref[0]), d.mid)


def build_kernel(d, flip_ref, taps_ref, dep_ref, inner_ref, mid_ref, outer_ref, y_ref, z_ref):
    h, mid, n = d.h, d.mid, d.nx
    for layer in range(z_ref.shape[0]):
        tap_x = x_taps(d, flip_ref, taps_ref, layer)
        inner_ref[layer] = banded(d, tap_x, lambda m: h + mid + m, lambda p: jnp.where(p < mid + h, h + p, 2 * n - 1 - p), h)
        mid_ref[layer] = banded(d, tap_x, lambda m: h + m, lambda p: p, mid)
        outer_ref[layer] = banded(d, tap_x, lambda m: m, lambda p: jnp.where(p < h, -1 - p, p - h), h)
        y_ref[layer] = banded(d, lambda t: taps_ref[layer, 1, t], lambda m: h + m, lambda p: p, mid)
        zr = lax.broadcasted_iota(jnp.int32, (d.nz, d.nz), 0)
        zs = lax.broadcasted_iota(jnp.int32, (d.nz, d.nz), 1)
        acc = jnp.zeros((d.nz, d.nz), F32)
        for t in range(d.taps):
            acc = jnp.where(zs - zr + d.h == t, taps_ref[layer, 2, t], acc)
        z_ref[layer] = acc.astype(BF)


def build_first(d, flip, taps):
    return pl.pallas_call(
        functools.partial(first_kernel, d),
        out_shape=jax.ShapeDtypeStruct((d.mid * ZB, (2 * d.h + d.mid) * ZB), BF),
        in_specs=[pl.BlockSpec(memory_space=pltpu.SMEM)] * 2,
        out_specs=pl.BlockSpec(memory_space=pltpu.VMEM),
        name="band_first",
        **params(2e5),
    )(flip, taps)


def build_bands(d, dep, flip, taps):
    n_layers = taps.shape[0]
    cols = (2 * d.h + d.mid) * ZB
    shapes = [(d.h * ZB, cols), (d.mid * ZB, cols), (d.h * ZB, cols), (d.mid * ZB, cols), (d.nz, d.nz)]
    return pl.pallas_call(
        functools.partial(build_kernel, d),
        out_shape=[jax.ShapeDtypeStruct((n_layers,) + s, BF) for s in shapes],
        in_specs=[pl.BlockSpec(memory_space=pltpu.SMEM)] * 2 + [pl.BlockSpec(memory_space=pl.ANY)],
        out_specs=[pl.BlockSpec(memory_space=pltpu.VMEM)] * len(shapes),
        name="bands",
        **params(1e6),
    )(flip, taps, dep)


def lane_block(d, n_rows):
    return lax.broadcasted_iota(jnp.int32, (n_rows, d.cm), 1) // d.cr


def pack_rest(d, spread):
    step = d.nz // d.rep
    blk = lane_block(d, step)
    out = spread[0:step]
    for q in range(1, d.rep):
        out = jnp.where(blk == q, spread[q * step:(q + 1) * step], out)
    return out


def spread_matrix(d):
    m = lax.broadcasted_iota(jnp.int32, (d.cr, d.cm), 0)
    n = lax.broadcasted_iota(jnp.int32, (d.cr, d.cm), 1)
    return jnp.where(n % d.cr == m, 1.0, 0.0).astype(BF)


def place(d, refs, y):
    if len(refs) == 1:
        return refs[0], y
    if d.h <= y < d.h + d.mid:
        return refs[1], y - d.h
    return refs[0], y if y < d.h else y - d.mid


def chunk_shapes(d, n, split):
    return [(n, c, d.rows, d.cm) for c in ((2 * d.h, d.mid) if split else (d.ny,))]


def pack_kernel(d, flip_ref, v_ref, dep_ref, *o_refs):
    spread_mat = spread_matrix(d)
    for y in range(d.ny):
        o_ref, col = place(d, o_refs, y)
        o_ref[0, col, 0:d.nz, :] = v_ref[0, y, :, 0:d.cm]
        rest = v_ref[0, y, :, d.cm:d.c]
        spread = jnp.dot(rest, spread_mat, preferred_element_type=F32)
        o_ref[0, col, d.nz:d.rows, :] = pack_rest(d, spread).astype(BF)


def mirrored(d, u, flip):
    return u + flip * (d.nx - 1 - 2 * u)


def pack(d, dep, flip, vol, u0, n, split=False):
    shapes = chunk_shapes(d, n, split)
    return pl.pallas_call(
        functools.partial(pack_kernel, d),
        out_shape=[jax.ShapeDtypeStruct(s, BF) for s in shapes],
        grid_spec=pltpu.PrefetchScalarGridSpec(
            num_scalar_prefetch=1,
            grid=(n,),
            in_specs=[
                pl.BlockSpec((1, d.ny, d.nz, d.c), lambda i, f: (mirrored(d, u0 + i, f[0]), 0, 0, 0)),
                pl.BlockSpec(memory_space=pl.ANY),
            ],
            out_specs=[pl.BlockSpec((1,) + s[1:], lambda i, f: (i, 0, 0, 0)) for s in shapes],
        ),
        name="pack",
        **params(n * 2.2e6),
    )(flip, vol, dep)


def xfilt_kernel(d, jobs, n_ins, n_mats, *refs):
    mats = [r[...] for r in refs[:n_mats]]
    ins = refs[n_mats:n_mats + n_ins]
    outs = refs[n_mats + n_ins + 1:]
    for out, (mat, planes) in zip(outs, jobs):
        n_out = out.shape[0]
        for s in range(d.slabs):
            sl = slice(s * ZB, (s + 1) * ZB)
            rhs = jnp.concatenate([ins[p][:, 0, sl, :].reshape(ins[p].shape[0] * ZB, d.cm) for p in planes], axis=0)
            res = jnp.dot(mats[mat], rhs, preferred_element_type=F32)
            out[:, 0, sl, :] = res.astype(BF).reshape(n_out, ZB, d.cm)


def xfilt(d, dep, mats, ins, jobs, steps):
    in_specs = [pl.BlockSpec(m.shape, lambda i: (0, 0)) for m in mats]
    for a, y_of in ins:
        in_specs.append(pl.BlockSpec((a.shape[0], 1, d.rows, d.cm), lambda i, f=y_of: (0, f(i), 0, 0)))
    in_specs.append(pl.BlockSpec(memory_space=pl.ANY))
    n_outs = [mats[m].shape[0] // ZB for m, _ in jobs]
    moved = sum(a.shape[0] for a, _ in ins) + sum(n_outs)
    return pl.pallas_call(
        functools.partial(xfilt_kernel, d, jobs, len(ins), len(mats)),
        grid=(steps,),
        out_shape=[jax.ShapeDtypeStruct((n, steps, d.rows, d.cm), BF) for n in n_outs],
        in_specs=in_specs,
        out_specs=[pl.BlockSpec((n, 1, d.rows, d.cm), lambda i: (0, i, 0, 0)) for n in n_outs],
        name="xfilt",
        **params(steps * moved * 40960),
    )(*mats, *[a for a, _ in ins], dep)


def columns(d, v, part):
    if len(v) == 2:
        return {"lo": (v[0], lambda i: i), "hi": (v[0], lambda i: d.h + i), "mid": (v[1], lambda i: i)}[part]
    return v[0], {"lo": lambda i: i, "hi": lambda i: d.h + d.mid + i, "mid": lambda i: d.h + i}[part]


def xfilt_edges(d, dep, mat, trio):
    ins = [columns(d, v, "lo") for v in trio] + [columns(d, v, "hi") for v in trio]
    return xfilt(d, dep, [mat], ins, [(0, (0, 1, 2)), (0, (3, 4, 5))], d.h)


def xfilt_middle(d, dep, mats, vs, jobs):
    return xfilt(d, dep, mats, [columns(d, v, "mid") for v in vs], jobs, d.mid)


def direct_kernel(d, t_ref, lo_ref, hi_ref, lo_out, hi_out):
    spread_mat = spread_matrix(d)
    t_mat = t_ref[...]
    for v_ref, o_ref in ((lo_ref, lo_out), (hi_ref, hi_out)):
        rest = v_ref[:, 0, :, d.cm:d.c].reshape(d.nx * d.nz, d.cr)
        spread = jnp.dot(rest, spread_mat, preferred_element_type=F32)
        packed = [pack_rest(d, spread[p * d.nz:(p + 1) * d.nz]).astype(BF) for p in range(d.nx)]
        for s in range(d.slabs):
            sl = slice(s * ZB, (s + 1) * ZB)
            if s * ZB < d.nz:
                rhs = v_ref[:, 0, sl, 0:d.cm].reshape(d.nx * ZB, d.cm)
            else:
                r0 = s * ZB - d.nz
                rhs = jnp.concatenate([p[r0:r0 + ZB] for p in packed], axis=0)
            res = jnp.dot(t_mat, rhs, preferred_element_type=F32)
            o_ref[:, 0, sl, :] = res.astype(BF).reshape(d.mid, ZB, d.cm)


def direct_edges(d, mat, vol):
    block = (d.nx, 1, d.nz, d.c)
    out = jax.ShapeDtypeStruct((d.mid, d.h, d.rows, d.cm), BF)
    return pl.pallas_call(
        functools.partial(direct_kernel, d),
        grid=(d.h,),
        out_shape=[out, out],
        in_specs=[
            pl.BlockSpec(mat.shape, lambda i: (0, 0)),
            pl.BlockSpec(block, lambda i: (0, i, 0, 0)),
            pl.BlockSpec(block, lambda i: (0, d.h + d.mid + i, 0, 0)),
        ],
        out_specs=[pl.BlockSpec((d.mid, 1, d.rows, d.cm), lambda i: (0, i, 0, 0))] * 2,
        name="direct",
        **params(4e7),
    )(mat, vol, vol)


def gelu(x):
    return x * (0.5 * (1.0 + jnp.tanh(0.7978845608028654 * (x + 0.044715 * (x * x * x)))))


def tail_kernel(d, last, n_v, flip_ref, t_ref, z_ref, wm_ref, wr_ref, b_ref, hl, lo, mi, hi, hr, *more):
    v_refs = more[:n_v]
    um_ref, ur_ref = more[-2:]
    o_refs = more[-3:-2] if last else more[-2 - n_v:-2]
    h, step = d.h, d.nz // d.rep
    parts = (
        (0, h, slice(0, h * ZB), (hl, lo, mi)),
        (h, d.mid, slice(0, d.mid * ZB), (lo, mi, hi)),
        (h + d.mid, h, slice((d.mid - h) * ZB, d.mid * ZB), (mi, hi, hr)),
    )
    z_mat = z_ref[...]
    b_main = b_ref[0:1, :]
    b_rest = b_ref[1:2, :]
    for y0, n, rows, trio in parts:
        t_mat = t_ref[rows, :]
        for s in range(d.slabs):
            sl = slice(s * ZB, (s + 1) * ZB)
            rhs = jnp.concatenate([r[0, :, sl, :].reshape(r.shape[1] * ZB, d.cm) for r in trio], axis=0)
            res = jnp.dot(t_mat, rhs, preferred_element_type=F32)
            if s * ZB < d.nz:
                um_ref[y0:y0 + n, sl, :] = res.astype(BF).reshape(n, ZB, d.cm)
            else:
                r0 = s * ZB - d.nz
                for q in range(d.rep):
                    piece = res[:, q * d.cr:(q + 1) * d.cr].astype(BF).reshape(n, ZB, d.cr)
                    ur_ref[y0:y0 + n, q * step + r0:q * step + r0 + ZB, :] = piece
    mains, rests = [], []
    for y in range(d.ny):
        mains.append(jnp.dot(z_mat, um_ref[y], preferred_element_type=F32).astype(BF))
        rests.append(jnp.dot(z_mat, ur_ref[y], preferred_element_type=F32).astype(BF))
    um = jnp.concatenate(mains, axis=0)
    ur = jnp.concatenate(rests, axis=0)
    main = jnp.dot(um, wm_ref[:, 0:d.cm], preferred_element_type=F32) + jnp.dot(ur, wr_ref[:, 0:d.cm], preferred_element_type=F32)
    rest = jnp.dot(um, wm_ref[:, d.cm:], preferred_element_type=F32) + jnp.dot(ur, wr_ref[:, d.cm:], preferred_element_type=F32)
    for y in range(d.ny):
        v_ref, col = place(d, v_refs, y)
        m = gelu(main[y * d.nz:(y + 1) * d.nz] + b_main) + v_ref[0, col, 0:d.nz, :].astype(F32)
        r = gelu(pack_rest(d, rest[y * d.nz:(y + 1) * d.nz]) + b_rest) + v_ref[0, col, d.nz:d.rows, :].astype(F32)
        o_ref, col = place(d, o_refs, y)
        if last:
            o_ref[0, y, :, 0:d.cm] = m.astype(BF)
            for q in range(d.rep):
                o_ref[0, y, q * step:(q + 1) * step, d.cm:d.c] = r[:, q * d.cr:(q + 1) * d.cr].astype(BF)
        else:
            o_ref[0, col, 0:d.nz, :] = m.astype(BF)
            o_ref[0, col, d.nz:d.rows, :] = r.astype(BF)


def tail(d, dep, flip, consts, us, v, last=False, u0=0, out_buf=None):
    n = v[0].shape[0]
    blocks = list(us) + list(v)
    in_specs = [pl.BlockSpec(a.shape, lambda i, f: (0, 0)) for a in consts]
    in_specs += [pl.BlockSpec((1,) + a.shape[1:], lambda i, f: (i, 0, 0, 0)) for a in blocks]
    args = [flip] + list(consts) + blocks + [dep]
    in_specs.append(pl.BlockSpec(memory_space=pl.ANY))
    alias = {}
    if last:
        out_shape = [jax.ShapeDtypeStruct((d.nx, d.ny, d.nz, d.c), BF)]
        out_specs = [pl.BlockSpec((1, d.ny, d.nz, d.c), lambda i, f: (mirrored(d, u0 + i, f[0]), 0, 0, 0))]
        if out_buf is not None:
            alias = {len(args): 0}
            args.append(out_buf)
            in_specs.append(pl.BlockSpec(memory_space=pl.ANY))
    else:
        shapes = chunk_shapes(d, n, len(v) == 2)
        out_shape = [jax.ShapeDtypeStruct(s, BF) for s in shapes]
        out_specs = [pl.BlockSpec((1,) + s[1:], lambda i, f: (i, 0, 0, 0)) for s in shapes]
    return pl.pallas_call(
        functools.partial(tail_kernel, d, last, len(v)),
        out_shape=out_shape,
        grid_spec=pltpu.PrefetchScalarGridSpec(
            num_scalar_prefetch=1,
            grid=(n,),
            in_specs=in_specs,
            out_specs=out_specs,
            scratch_shapes=[pltpu.VMEM((d.ny, d.nz, d.cm), BF), pltpu.VMEM((d.ny, d.nz, d.cr), BF)],
        ),
        input_output_aliases=alias,
        name="tail",
        **params(n * 3.6e6),
    )(*args)


def solution(mesh):
    x_count = mesh.shape[ROW_AXIS]
    y_count = mesh.shape[COL_AXIS]
    vol_spec = P(PARTS_AXIS, ROW_AXIS, COL_AXIS, None)

    def swap(a, first):
        pairs = [(s, s + 1) for s in range(first, x_count - 1, 2)]
        return lax.ppermute(a, ROW_AXIS, pairs + [(b, a_) for a_, b in pairs])

    def swap_out(v):
        return [swap(v[0], 1), swap(v[1], 1)]

    def share(lo, hi):
        below = lax.ppermute(hi, COL_AXIS, [(s, s + 1) for s in range(y_count - 1)])
        above = lax.ppermute(lo, COL_AXIS, [(s + 1, s) for s in range(y_count - 1)])
        return below, above

    def local_layers(volume, filter_taps, mix_weights, mix_bias):
        n_layers = filter_taps.shape[0]
        d = Dims(volume.shape, filter_taps.shape[-1])
        h, mid = d.h, d.mid
        two = [(0, (0, 1, 2)), (1, (1, 2, 3))]
        one = [(0, (0, 1, 2))]
        flip = (lax.axis_index(ROW_AXIS) % 2).astype(jnp.int32).reshape(1)
        vol = jnp.transpose(volume, (1, 2, 3, 0))
        t_first = build_first(d, flip, filter_taps)
        lo_mid, hi_mid = direct_edges(d, t_first, vol)
        s_mid = share(lo_mid, hi_mid)
        v_in = pack(d, lo_mid, flip, vol, h + mid, h)
        h_in = [swap(v_in[0], 0)]
        v_out = pack(d, v_in[0], flip, vol, 0, h, True)
        h_out = swap_out(v_out)
        v_mid = pack(d, v_out[0], flip, vol, h, mid)
        t_in, t_mid, t_out, t_y, t_z = build_bands(d, v_mid[0], flip, filter_taps)
        w_ext = jnp.concatenate([mix_weights[:, :, :d.cm]] + [mix_weights[:, :, d.cm:]] * d.rep, axis=2)
        bias = jnp.stack([mix_bias[:, :d.cm], jnp.concatenate([mix_bias[:, d.cm:]] * d.rep, axis=1)], axis=1)
        lo_in, hi_in = xfilt_edges(d, v_mid[0], t_in[0], (v_mid, v_in, h_in))
        s_in = share(lo_in, hi_in)
        dep = lo_in
        res = None
        for layer in range(n_layers):
            first, last = layer == 0, layer == n_layers - 1
            consts = (t_y[layer], t_z[layer], w_ext[layer, :d.cm], w_ext[layer, d.cm:], bias[layer])

            def run_tail(dep, halos, lo, m, hi, v, u0, out_buf=None):
                us = (halos[0], lo, m, hi, halos[1])
                return tail(d, dep, flip, consts, us, v, last, u0, out_buf)

            if not first:
                h_out = swap_out(v_out)
                lo_mid, hi_mid = xfilt_edges(d, dep, t_mid[layer], (v_out, v_mid, v_in))
                s_mid = share(lo_mid, hi_mid)
                dep = lo_mid
            m_mid, m_in = xfilt_middle(d, dep, [t_mid[layer], t_in[layer]], (v_out, v_mid, v_in, h_in), two)
            out_trio = (h_out, v_out, v_mid)
            if first:
                w_mid = run_tail(m_mid, s_mid, lo_mid, m_mid, hi_mid, v_mid, h)
                lo_out, hi_out = xfilt_edges(d, w_mid[0], t_out[layer], out_trio)
                s_out = share(lo_out, hi_out)
                w_in = run_tail(lo_out, s_in, lo_in, m_in, hi_in, v_in, h + mid)
                h_in = [swap(w_in[0], 0)]
                (m_out,) = xfilt_middle(d, w_in[0], [t_out[layer]], out_trio, one)
            else:
                w_in = run_tail(m_mid, s_in, lo_in, m_in, hi_in, v_in, h + mid)
                if not last:
                    h_in = [swap(w_in[0], 0)]
                lo_out, hi_out = xfilt_edges(d, w_in[0], t_out[layer], out_trio)
                s_out = share(lo_out, hi_out)
                (m_out,) = xfilt_middle(d, lo_out, [t_out[layer]], out_trio, one)
                w_mid = run_tail(m_out, s_mid, lo_mid, m_mid, hi_mid, v_mid, h, w_in[0] if last else None)
            if last:
                (res,) = run_tail(m_out, s_out, lo_out, m_out, hi_out, v_out, 0, w_mid[0])
                break
            dep = m_out if first else w_mid[0]
            lo_in, hi_in = xfilt_edges(d, dep, t_in[layer + 1], (w_mid, w_in, h_in))
            s_in = share(lo_in, hi_in)
            w_out = run_tail(lo_in, s_out, lo_out, m_out, hi_out, v_out, 0)
            v_in, v_mid, v_out = w_in, w_mid, w_out
            dep = w_out[0]
        return jnp.transpose(res, (3, 0, 1, 2))

    return jax.shard_map(local_layers, mesh=mesh, in_specs=(vol_spec, P(), P(), P()), out_specs=vol_spec, check_vma=False)
```

time: 651 us -> 615 us (0.945)
  waiting for transfers between devices: 171 us -> 126 us
  starting transfers between devices: 59.2 us -> 76.2 us
    ppermute x9, waiting for transfers between devices: 56.1 us -> 20.6 us  [share(): above = lax.ppermute(lo, COL_AXIS, [(s + 1, s) for s in range(y_count - 1)])]
    pallas_call x12 -> x14, Pallas kernels: 229 us -> 245 us  [the longest x9 198 us: tail(): pl.pallas_call(functools.partial(tail_kernel, d, last, len(v)), out_shape...]
    ppermute x9, waiting for transfers between devices: 37 us -> 24.9 us  [share(): below = lax.ppermute(hi, COL_AXIS, [(s, s + 1) for s in range(y_count - 1)])]
    pallas_call x15 -> x14, Pallas kernels: 159 us -> 148 us  [xfilt(): pl.pallas_call(functools.partial(xfilt_kernel, d, jobs, len(ins), len(mat...]
    ppermute x9, starting transfers between devices: 35.2 us -> 45 us  [share(): below = lax.ppermute(hi, COL_AXIS, [(s, s + 1) for s in range(y_count - 1)])]
    ppermute x6 -> x9, starting transfers between devices: 11.8 us -> 19.3 us  [swap(): return lax.ppermute(a, ROW_AXIS, pairs + [(b, a_) for a_, b in pairs])]
    ppermute x6 -> x9, waiting for transfers between devices: 78.2 us -> 80.9 us  [swap(): return lax.ppermute(a, ROW_AXIS, pairs + [(b, a_) for a_, b in pairs])]
  transfers between devices with their start and end apart: 24 -> 27, of which waited for: 13 -> 11; matrix products, arithmetic and copies ran while one was open for 3% -> 2% of each run, Pallas kernels for 52% -> 48%
where the time goes in v1:
time: 615 us; the launch traced here: 611 us
  Pallas kernels  396 us (64%)
  waiting for transfers between devices  126 us (20%)
  starting transfers between devices  76.2 us (12%)
  local copies, waits for them, and re-layouts  7.84 us (1%)
    pallas_call x9, Pallas kernels, tail(): pl.pallas_call(functools.partial(tail_kernel, d, last, len(v)), out_shape...  198 us
    pallas_call x14, Pallas kernels, xfilt(): pl.pallas_call(functools.partial(xfilt_kernel, d, jobs, len(ins), len(mat...  148 us
    ppermute x9, waiting for transfers between devices, swap(): return lax.ppermute(a, ROW_AXIS, pairs + [(b, a_) for a_, b in pairs])  80.9 us
    ppermute x9, starting transfers between devices, share(): below = lax.ppermute(hi, COL_AXIS, [(s, s + 1) for s in range(y_count - 1)])  45 us
    pallas_call x3, Pallas kernels, pack(): pl.pallas_call(functools.partial(pack_kernel, d), out_shape=[jax.ShapeDty...  31.6 us
    ppermute x9, waiting for transfers between devices, share(): below = lax.ppermute(hi, COL_AXIS, [(s, s + 1) for s in range(y_count - 1)])  24.9 us
    ppermute x9, waiting for transfers between devices, share(): above = lax.ppermute(lo, COL_AXIS, [(s + 1, s) for s in range(y_count - 1)])  20.6 us
    ppermute x9, starting transfers between devices, swap(): return lax.ppermute(a, ROW_AXIS, pairs + [(b, a_) for a_, b in pairs])  19.3 us
  transfers between devices with their start and end apart: 27, of which 11 were waited for; matrix products, arithmetic and copies ran while one was open for 2% of the time, Pallas kernels for 48%

profile of v1, /device:TPU:1, one launch (start us, length us, event | category | flops | bytes accessed | tf_op | source)
XLA Modules:
  0.0 610.8 jit_solution(17185037596054558632)
XLA Ops:
  1.7 12.9 %direct.1 = (bf16[10,7,80,256]{3,2,1,0:T(8,128)(2,1)}, bf16[10,7,80,256]{3,2,1,0:T(8,128)(2,1)}) custom-call(bf16[160,384]{1,0:T(8,128)(2,1)} %band_first.1.t_ref, bf16[24,24,64,320]{3,2,1,0:T(8,128)(2,1)} %bitcast.51, bf16[24,24,64,320]{3,2,1,0:T(8,128)(2,1)} %bitcast.52), custom_call_target="tpu_custom_call" | custom-call | bytes 40000000 | tf_op jit(solution)/shard_map/direct/pallas_call | solution.py:232
  14.6 9.7 %pack.3.dep_ref.refs_2_.refs_5_.refs_4_.more_0_ = bf16[7,24,80,256]{3,2,1,0:T(8,128)(2,1)} custom-call(s32[1]{0:T(128)} %bitcast.flip_ref, bf16[24,24,64,320]{3,2,1,0:T(8,128)(2,1)} %bitcast.53, bf16[10,7,80,256]{3,2,1,0:T(8,128)(2,1)} %get-tuple-element.40.dep_ref.lo), custom_call_target="tpu_custom_call" | custom-call | bytes 15400000 | tf_op jit(solution)/shard_map/pack/pallas_call | solution.py:148
  24.3 9.5 %pack.4 = (bf16[7,14,80,256]{3,2,1,0:T(8,128)(2,1)}, bf16[7,10,80,256]{3,2,1,0:T(8,128)(2,1)}) custom-call(s32[1]{0:T(128)} %bitcast.flip_ref, bf16[24,24,64,320]{3,2,1,0:T(8,128)(2,1)} %bitcast.54, bf16[7,24,80,256]{3,2,1,0:T(8,128)(2,1)} %pack.3.dep_ref.refs_2_.refs_5_.refs_4_.more_0_), custom_call_target="tpu_custom_call" | custom-call | bytes 15400000 | tf_op jit(solution)/shard_map/pack/pallas_call | solution.py:148
  44.5 12.4 %pack.5.dep_ref.refs_1_.refs_4_.refs_7_.refs_3_.more_0_.refs_6_ = bf16[10,24,80,256]{3,2,1,0:T(8,128)(2,1)} custom-call(s32[1]{0:T(128)} %bitcast.flip_ref, bf16[24,24,64,320]{3,2,1,0:T(8,128)(2,1)} %bitcast.55, bf16[7,14,80,256]{3,2,1,0:T(8,128)(2,1)} %get-tuple-element.41.dep_ref.refs_2_.refs_5_.more_0_), custom_call_target="tpu_custom_call" | custom-call | bytes 22000000 | tf_op jit(solution)/shard_map/pack/pallas_call | solution.py:148
  62.8 10.1 %xfilt.14 = (bf16[7,7,80,256]{3,2,1,0:T(8,128)(2,1)}, bf16[7,7,80,256]{3,2,1,0:T(8,128)(2,1)}) custom-call(bf16[112,384]{1,0:T(8,128)(2,1)} %get-tuple-element.89.refs_0_.refs_1_, bf16[10,24,80,256]{3,2,1,0:T(8,128)(2,1)} %pack.5.dep_ref.refs_1_.refs_4_.refs_7_.refs_3_.more_0_.refs_6_, bf16[7,24,80,256]{3,2,1,0:T(8,128)(2,1)} %pack.3.dep_ref.refs_2_.refs_5_.refs_4_.more_0_, ...), custom_call_target="tpu_custom_call" | custom-call | bytes 17776640 | tf_op jit(solution)/shard_map/xfilt/pallas_call | solution.py:185
  89.8 12.0 %xfilt.15 = (bf16[10,10,80,256]{3,2,1,0:T(8,128)(2,1)}, bf16[7,10,80,256]{3,2,1,0:T(8,128)(2,1)}) custom-call(bf16[160,384]{1,0:T(8,128)(2,1)} %get-tuple-element.83.refs_0_, bf16[112,384]{1,0:T(8,128)(2,1)} %get-tuple-element.89.refs_0_.refs_1_, bf16[7,10,80,256]{3,2,1,0:T(8,128)(2,1)} %get-tuple-element.48.refs_2_.more_1_, ...), custom_call_target="tpu_custom_call" | custom-call | bytes 19660800 | tf_op jit(solution)/shard_map/xfilt/pallas_call | solution.py:185
  109.2 26.5 %tail.9.refs_7_.refs_1_.refs_4_.refs_2_.refs_5_.refs_3_.refs_6_.more_0_ = bf16[10,24,80,256]{3,2,1,0:T(8,128)(2,1)} custom-call(s32[1]{0:T(128)} %bitcast.flip_ref, bf16[160,384]{1,0:T(8,128)(2,1)} %get-tuple-element.84.t_ref, bf16[64,64]{1,0:T(8,128)(2,1)} %get-tuple-element.93.z_ref, bf16[256,512]{1,0:T(8,128)(2,1)} %get-tuple-element.78.wm_ref, ...), custom_call_target="tpu_custom_call" | custom-call | bytes 36000000 | tf_op jit(solution)/shard_map/tail/pallas_call | solution.py:318
  135.7 10.1 %xfilt.16 = (bf16[7,7,80,256]{3,2,1,0:T(8,128)(2,1)}, bf16[7,7,80,256]{3,2,1,0:T(8,128)(2,1)}) custom-call(bf16[112,384]{1,0:T(8,128)(2,1)} %get-tuple-element.90.refs_0_, bf16[7,14,80,256]{3,2,1,0:T(8,128)(2,1)} %collective-permute-done.refs_1_.refs_4_, bf16[7,14,80,256]{3,2,1,0:T(8,128)(2,1)} %get-tuple-element.41.dep_ref.refs_2_.refs_5_.more_0_, ...), custom_call_target="tpu_custom_call" | custom-call | bytes 17776640 | tf_op jit(solution)/shard_map/xfilt/pallas_call | solution.py:185
  152.2 19.4 %tail.10.refs_4_.refs_2_.refs_5_.refs_3_.refs_6_.more_0_ = bf16[7,24,80,256]{3,2,1,0:T(8,128)(2,1)} custom-call(s32[1]{0:T(128)} %bitcast.flip_ref, bf16[160,384]{1,0:T(8,128)(2,1)} %get-tuple-element.84.t_ref, bf16[64,64]{1,0:T(8,128)(2,1)} %get-tuple-element.93.z_ref, bf16[256,512]{1,0:T(8,128)(2,1)} %get-tuple-element.78.wm_ref, ...), custom_call_target="tpu_custom_call" | custom-call | bytes 25200000 | tf_op jit(solution)/shard_map/tail/pallas_call | solution.py:318
  179.2 29.4 %collective-permute-done.5.refs_1_ = bf16[7,10,80,256]{3,2,1,0:T(8,128)(2,1)} collective-permute-done((bf16[7,10,80,256]{3,2,1,0:T(8,128)(2,1)}, bf16[7,10,80,256]{3,2,1,0:T(8,128)(2,1)}, u32[]{:S(2)}, u32[]{:S(2)}) %collective-permute-start.5) | collective-permute-done | bytes 2867232 | tf_op jit(solution)/shard_map/ppermute | solution.py:341
  208.6 9.6 %xfilt.17.refs_7_.mi = bf16[7,10,80,256]{3,2,1,0:T(8,128)(2,1)} custom-call(bf16[112,384]{1,0:T(8,128)(2,1)} %get-tuple-element.90.refs_0_, bf16[7,10,80,256]{3,2,1,0:T(8,128)(2,1)} %collective-permute-done.5.refs_1_, bf16[7,10,80,256]{3,2,1,0:T(8,128)(2,1)} %get-tuple-element.48.refs_2_.more_1_, ...), custom_call_target="tpu_custom_call" | custom-call | bytes 12697600 | tf_op jit(solution)/shard_map/xfilt/pallas_call | solution.py:185
  218.2 10.1 %xfilt.18 = (bf16[7,7,80,256]{3,2,1,0:T(8,128)(2,1)}, bf16[7,7,80,256]{3,2,1,0:T(8,128)(2,1)}) custom-call(bf16[112,384]{1,0:T(8,128)(2,1)} %get-tuple-element.88.refs_0_.refs_1_, bf16[10,24,80,256]{3,2,1,0:T(8,128)(2,1)} %tail.9.refs_7_.refs_1_.refs_4_.refs_2_.refs_5_.refs_3_.refs_6_.more_0_, ...), custom_call_target="tpu_custom_call" | custom-call | bytes 17776640 | tf_op jit(solution)/shard_map/xfilt/pallas_call | solution.py:185
  232.7 19.5 %tail.11 = (bf16[7,14,80,256]{3,2,1,0:T(8,128)(2,1)}, bf16[7,10,80,256]{3,2,1,0:T(8,128)(2,1)}) custom-call(s32[1]{0:T(128)} %bitcast.flip_ref, bf16[160,384]{1,0:T(8,128)(2,1)} %get-tuple-element.84.t_ref, bf16[64,64]{1,0:T(8,128)(2,1)} %get-tuple-element.93.z_ref, bf16[256,512]{1,0:T(8,128)(2,1)} %get-tuple-element.78.wm_ref, ...), custom_call_target="tpu_custom_call" | custom-call | bytes 25200000 | tf_op jit(solution)/shard_map/tail/pallas_call | solution.py:318
  252.3 11.1 %xfilt.19 = (bf16[10,7,80,256]{3,2,1,0:T(8,128)(2,1)}, bf16[10,7,80,256]{3,2,1,0:T(8,128)(2,1)}) custom-call(bf16[160,384]{1,0:T(8,128)(2,1)} %get-tuple-element.82.refs_0_, bf16[7,14,80,256]{3,2,1,0:T(8,128)(2,1)} %get-tuple-element.56.refs_1_.refs_4_.refs_7_.refs_2_.refs_5_.more_0_, ...), custom_call_target="tpu_custom_call" | custom-call | bytes 19496960 | tf_op jit(solution)/shard_map/xfilt/pallas_call | solution.py:185
  263.3 12.0 %xfilt.20 = (bf16[10,10,80,256]{3,2,1,0:T(8,128)(2,1)}, bf16[7,10,80,256]{3,2,1,0:T(8,128)(2,1)}) custom-call(bf16[160,384]{1,0:T(8,128)(2,1)} %get-tuple-element.82.refs_0_, bf16[112,384]{1,0:T(8,128)(2,1)} %get-tuple-element.88.refs_0_.refs_1_, bf16[7,10,80,256]{3,2,1,0:T(8,128)(2,1)} %get-tuple-element.58.refs_2_.more_1_, ...), custom_call_target="tpu_custom_call" | custom-call | bytes 19660800 | tf_op jit(solution)/shard_map/xfilt/pallas_call | solution.py:185
  275.3 19.5 %tail.12.refs_7_.refs_2_.refs_5_.refs_3_.refs_6_.refs_4_.more_0_ = bf16[7,24,80,256]{3,2,1,0:T(8,128)(2,1)} custom-call(s32[1]{0:T(128)} %bitcast.flip_ref, bf16[160,384]{1,0:T(8,128)(2,1)} %get-tuple-element.85.t_ref, bf16[64,64]{1,0:T(8,128)(2,1)} %get-tuple-element.94.z_ref, bf16[256,512]{1,0:T(8,128)(2,1)} %get-tuple-element.79.wm_ref, ...), custom_call_target="tpu_custom_call" | custom-call | bytes 25200000 | tf_op jit(solution)/shard_map/tail/pallas_call | solution.py:318
  307.2 36.1 %collective-permute-done.10.refs_1_.refs_4_ = bf16[7,14,80,256]{3,2,1,0:T(8,128)(2,1)} collective-permute-done((bf16[7,14,80,256]{3,2,1,0:T(8,128)(2,1)}, bf16[7,14,80,256]{3,2,1,0:T(8,128)(2,1)}, u32[]{:S(2)}, u32[]{:S(2)}) %collective-permute-start.10) | collective-permute-done | bytes 4014112 | tf_op jit(solution)/shard_map/ppermute | solution.py:341
  343.4 10.1 %xfilt.21 = (bf16[7,7,80,256]{3,2,1,0:T(8,128)(2,1)}, bf16[7,7,80,256]{3,2,1,0:T(8,128)(2,1)}) custom-call(bf16[112,384]{1,0:T(8,128)(2,1)} %get-tuple-element.91.refs_0_, bf16[7,14,80,256]{3,2,1,0:T(8,128)(2,1)} %collective-permute-done.10.refs_1_.refs_4_, bf16[7,14,80,256]{3,2,1,0:T(8,128)(2,1)} %get-tuple-element.56.refs_1_.refs_4_.refs_7_.refs_2_.refs_5_.more_0_, ...), custom_call_target="tpu_custom_call" | custom-call | bytes 17776640 | tf_op jit(solution)/shard_map/xfilt/pallas_call | solution.py:185
  358.7 15.3 %collective-permute-done.14.refs_1_ = bf16[7,10,80,256]{3,2,1,0:T(8,128)(2,1)} collective-permute-done((bf16[7,10,80,256]{3,2,1,0:T(8,128)(2,1)}, bf16[7,10,80,256]{3,2,1,0:T(8,128)(2,1)}, u32[]{:S(2)}, u32[]{:S(2)}) %collective-permute-start.14) | collective-permute-done | bytes 2867232 | tf_op jit(solution)/shard_map/ppermute | solution.py:341
  375.4 9.6 %xfilt.22.more_1_.mi = bf16[7,10,80,256]{3,2,1,0:T(8,128)(2,1)} custom-call(bf16[112,384]{1,0:T(8,128)(2,1)} %get-tuple-element.91.refs_0_, bf16[7,10,80,256]{3,2,1,0:T(8,128)(2,1)} %collective-permute-done.14.refs_1_, bf16[7,10,80,256]{3,2,1,0:T(8,128)(2,1)} %get-tuple-element.58.refs_2_.more_1_, ...), custom_call_target="tpu_custom_call" | custom-call | bytes 12697600 | tf_op jit(solution)/shard_map/xfilt/pallas_call | solution.py:185
  385.0 26.6 %tail.13.refs_1_.refs_4_.refs_7_.refs_2_.refs_5_.refs_3_.refs_6_.more_0_ = bf16[10,24,80,256]{3,2,1,0:T(8,128)(2,1)} custom-call(s32[1]{0:T(128)} %bitcast.flip_ref, bf16[160,384]{1,0:T(8,128)(2,1)} %get-tuple-element.85.t_ref, bf16[64,64]{1,0:T(8,128)(2,1)} %get-tuple-element.94.z_ref, bf16[256,512]{1,0:T(8,128)(2,1)} %get-tuple-element.79.wm_ref, ...), custom_call_target="tpu_custom_call" | custom-call | bytes 36000000 | tf_op jit(solution)/shard_map/tail/pallas_call | solution.py:318
  411.6 10.1 %xfilt.23 = (bf16[7,7,80,256]{3,2,1,0:T(8,128)(2,1)}, bf16[7,7,80,256]{3,2,1,0:T(8,128)(2,1)}) custom-call(bf16[112,384]{1,0:T(8,128)(2,1)} %get-tuple-element.87.refs_0_.refs_1_, bf16[10,24,80,256]{3,2,1,0:T(8,128)(2,1)} %tail.13.refs_1_.refs_4_.refs_7_.refs_2_.refs_5_.refs_3_.refs_6_.more_0_, ...), custom_call_target="tpu_custom_call" | custom-call | bytes 17776640 | tf_op jit(solution)/shard_map/xfilt/pallas_call | solution.py:185
  421.7 19.5 %tail.14 = (bf16[7,14,80,256]{3,2,1,0:T(8,128)(2,1)}, bf16[7,10,80,256]{3,2,1,0:T(8,128)(2,1)}) custom-call(s32[1]{0:T(128)} %bitcast.flip_ref, bf16[160,384]{1,0:T(8,128)(2,1)} %get-tuple-element.85.t_ref, bf16[64,64]{1,0:T(8,128)(2,1)} %get-tuple-element.94.z_ref, bf16[256,512]{1,0:T(8,128)(2,1)} %get-tuple-element.79.wm_ref, ...), custom_call_target="tpu_custom_call" | custom-call | bytes 25200000 | tf_op jit(solution)/shard_map/tail/pallas_call | solution.py:318
  443.8 6.3 %collective-permute-start.20 = (bf16[7,7,80,256]{3,2,1,0:T(8,128)(2,1)}, bf16[7,7,80,256]{3,2,1,0:T(8,128)(2,1)}, u32[]{:S(2)}, u32[]{:S(2)}) collective-permute-start(bf16[7,7,80,256]{3,2,1,0:T(8,128)(2,1)} %get-tuple-element.67.hi), channel_id=1, source_target_pairs={{0,4},{4,8},{8,12},{1,5},{5,9},{9,13},{2,6},{6,10},{10,14},{3,7},{... | collective-permute-start | bytes 6021128 | tf_op jit(solution)/shard_map/ppermute | solution.py:347
  454.6 11.1 %xfilt.24 = (bf16[10,7,80,256]{3,2,1,0:T(8,128)(2,1)}, bf16[10,7,80,256]{3,2,1,0:T(8,128)(2,1)}) custom-call(bf16[160,384]{1,0:T(8,128)(2,1)} %get-tuple-element.81.refs_0_, bf16[7,14,80,256]{3,2,1,0:T(8,128)(2,1)} %get-tuple-element.66.refs_1_.refs_4_.refs_7_.refs_2_.refs_5_.more_0_, ...), custom_call_target="tpu_custom_call" | custom-call | bytes 19496960 | tf_op jit(solution)/shard_map/xfilt/pallas_call | solution.py:185
  471.7 20.8 %collective-permute-done.20.hl = bf16[7,7,80,256]{3,2,1,0:T(8,128)(2,1)} collective-permute-done((bf16[7,7,80,256]{3,2,1,0:T(8,128)(2,1)}, bf16[7,7,80,256]{3,2,1,0:T(8,128)(2,1)}, u32[]{:S(2)}, u32[]{:S(2)}) %collective-permute-start.20) | collective-permute-done | bytes 2007072 | tf_op jit(solution)/shard_map/ppermute | solution.py:347
  493.8 12.0 %xfilt.25 = (bf16[10,10,80,256]{3,2,1,0:T(8,128)(2,1)}, bf16[7,10,80,256]{3,2,1,0:T(8,128)(2,1)}) custom-call(bf16[160,384]{1,0:T(8,128)(2,1)} %get-tuple-element.81.refs_0_, bf16[112,384]{1,0:T(8,128)(2,1)} %get-tuple-element.87.refs_0_.refs_1_, bf16[7,10,80,256]{3,2,1,0:T(8,128)(2,1)} %get-tuple-element.68.refs_2_.more_1_, ...), custom_call_target="tpu_custom_call" | custom-call | bytes 19660800 | tf_op jit(solution)/shard_map/xfilt/pallas_call | solution.py:185
  505.8 19.9 %tail.15.refs_7_.more_2_ = bf16[24,24,64,320]{3,2,1,0:T(8,128)(2,1)} custom-call(s32[1]{0:T(128)} %bitcast.flip_ref, bf16[160,384]{1,0:T(8,128)(2,1)} %get-tuple-element.86.t_ref, bf16[64,64]{1,0:T(8,128)(2,1)} %get-tuple-element.95.z_ref, bf16[256,512]{1,0:T(8,128)(2,1)} %get-tuple-element.80.wm_ref, bf16[64,512]{1,0:T(8,128)(2,1)} %get-tuple-element.76.wr_ref, ...), custom_call_target="tpu_custom_call" | custom-call | bytes 25200000 | tf_op jit(solution)/shard_map/tail/pallas_call | solution.py:318
  525.7 10.2 %xfilt.26 = (bf16[7,7,80,256]{3,2,1,0:T(8,128)(2,1)}, bf16[7,7,80,256]{3,2,1,0:T(8,128)(2,1)}) custom-call(bf16[112,384]{1,0:T(8,128)(2,1)} %get-tuple-element.92.refs_0_, bf16[7,14,80,256]{3,2,1,0:T(8,128)(2,1)} %collective-permute-done.19.refs_1_.refs_4_, bf16[7,14,80,256]{3,2,1,0:T(8,128)(2,1)} %get-tuple-element.66.refs_1_.refs_4_.refs_7_.refs_2_.refs_5_.more_0_, ...), custom_call_target="tpu_custom_call" | custom-call | bytes 17776640 | tf_op jit(solution)/shard_map/xfilt/pallas_call | solution.py:185
  543.2 9.6 %xfilt.27.more_1_.mi.more_2_ = bf16[7,10,80,256]{3,2,1,0:T(8,128)(2,1)} custom-call(bf16[112,384]{1,0:T(8,128)(2,1)} %get-tuple-element.92.refs_0_, bf16[7,10,80,256]{3,2,1,0:T(8,128)(2,1)} %collective-permute-done.23.refs_1_, bf16[7,10,80,256]{3,2,1,0:T(8,128)(2,1)} %get-tuple-element.68.refs_2_.more_1_, ...), custom_call_target="tpu_custom_call" | custom-call | bytes 12697600 | tf_op jit(solution)/shard_map/xfilt/pallas_call | solution.py:185
  559.6 27.1 %tail.16.more_3_ = bf16[24,24,64,320]{3,2,1,0:T(8,128)(2,1)} custom-call(s32[1]{0:T(128)} %bitcast.flip_ref, bf16[160,384]{1,0:T(8,128)(2,1)} %get-tuple-element.86.t_ref, bf16[64,64]{1,0:T(8,128)(2,1)} %get-tuple-element.95.z_ref, bf16[256,512]{1,0:T(8,128)(2,1)} %get-tuple-element.80.wm_ref, ...), custom_call_target="tpu_custom_call", output_to_operand_aliasing={{}: (13, {})} | custom-call | bytes 36000000 | tf_op jit(solution)/shard_map/tail/pallas_call | solution.py:318
  590.8 20.1 %tail.17 = bf16[24,24,64,320]{3,2,1,0:T(8,128)(2,1)} custom-call(s32[1]{0:T(128)} %bitcast.flip_ref, bf16[160,384]{1,0:T(8,128)(2,1)} %get-tuple-element.86.t_ref, bf16[64,64]{1,0:T(8,128)(2,1)} %get-tuple-element.95.z_ref, bf16[256,512]{1,0:T(8,128)(2,1)} %get-tuple-element.80.wm_ref, ...), custom_call_target="tpu_custom_call", output_to_operand_aliasing={{}: (14, {})} | custom-call | bytes 25200000 | tf_op jit(solution)/shard_map/tail/pallas_call | solution.py:318
  (74 shorter events, 112.2 us)
Async XLA Ops:
  24.3 38.4 %collective-permute-start.2 = (bf16[7,24,80,256]{3,2,1,0:T(8,128)(2,1)}, bf16[7,24,80,256]{3,2,1,0:T(8,128)(2,1)}, u32[]{:S(2)}, u32[]{:S(2)}) collective-permute-start(bf16[7,24,80,256]{3,2,1,0:T(8,128)(2,1)} %pack.3.dep_ref.refs_2_.refs_5_.refs_4_.more_0_), channel_id=1, source_target_pairs={{0,1},{2,3},{1,0},{3,2},{4,5},{6,7},{5,4},{7,6},{8,9},{10,11},{9,8... | collective-permute-start | bytes 20643848 | tf_op jit(solution)/shard_map/ppermute | solution.py:341
  33.9 101.9 %collective-permute-start = (bf16[7,14,80,256]{3,2,1,0:T(8,128)(2,1)}, bf16[7,14,80,256]{3,2,1,0:T(8,128)(2,1)}, u32[]{:S(2)}, u32[]{:S(2)}) collective-permute-start(bf16[7,14,80,256]{3,2,1,0:T(8,128)(2,1)} %get-tuple-element.41.dep_ref.refs_2_.refs_5_.more_0_), channel_id=1, source_target_pairs={{1,2},{2,1},{5,6},{6,5},{9,10},{10,9},{13,14},{14,13},{17,18},{18,... | collective-permute-start | bytes 12042248 | tf_op jit(solution)/shard_map/ppermute | solution.py:341
  38.4 65.4 %collective-permute-start.1 = (bf16[10,7,80,256]{3,2,1,0:T(8,128)(2,1)}, bf16[10,7,80,256]{3,2,1,0:T(8,128)(2,1)}, u32[]{:S(2)}, u32[]{:S(2)}) collective-permute-start(bf16[10,7,80,256]{3,2,1,0:T(8,128)(2,1)} %get-tuple-element.45.hi), channel_id=1, source_target_pairs={{0,4},{4,8},{8,12},{1,5},{5,9},{9,13},{2,6},{6,10},{10,14},{3,7},{... | collective-permute-start | bytes 8601608 | tf_op jit(solution)/shard_map/ppermute | solution.py:347
  43.2 66.0 %collective-permute-start.3 = (bf16[10,7,80,256]{3,2,1,0:T(8,128)(2,1)}, bf16[10,7,80,256]{3,2,1,0:T(8,128)(2,1)}, u32[]{:S(2)}, u32[]{:S(2)}) collective-permute-start(bf16[10,7,80,256]{3,2,1,0:T(8,128)(2,1)} %get-tuple-element.40.dep_ref.lo), channel_id=1, source_target_pairs={{4,0},{8,4},{12,8},{5,1},{9,5},{13,9},{6,2},{10,6},{14,10},{7,3},{... | collective-permute-start | bytes 8601608 | tf_op jit(solution)/shard_map/ppermute | solution.py:348
  72.9 13.1 %copy-start.3 = (bf16[3,64,64]{2,1,0:T(8,128)(2,1)S(1)}, bf16[3,64,64]{2,1,0:T(8,128)(2,1)}, u32[]{:S(2)}) copy-start(bf16[3,64,64]{2,1,0:T(8,128)(2,1)} %get-tuple-element.43) | copy-start | bytes 73732
  72.9 13.8 %copy-start.2 = (bf16[3,112,384]{2,1,0:T(8,128)(2,1)S(1)}, bf16[3,112,384]{2,1,0:T(8,128)(2,1)}, u32[]{:S(2)}) copy-start(bf16[3,112,384]{2,1,0:T(8,128)(2,1)} %get-tuple-element.44) | copy-start | bytes 774148
  72.9 14.4 %copy-start.1 = (bf16[3,160,384]{2,1,0:T(8,128)(2,1)S(1)}, bf16[3,160,384]{2,1,0:T(8,128)(2,1)}, u32[]{:S(2)}) copy-start(bf16[3,160,384]{2,1,0:T(8,128)(2,1)} %get-tuple-element.42) | copy-start | bytes 1105924
  72.9 15.2 %copy-start = (bf16[3,160,384]{2,1,0:T(8,128)(2,1)S(1)}, bf16[3,160,384]{2,1,0:T(8,128)(2,1)}, u32[]{:S(2)}) copy-start(bf16[3,160,384]{2,1,0:T(8,128)(2,1)} %get-tuple-element.46) | copy-start | bytes 1105924
  72.9 73.9 %collective-permute-start.6 = (bf16[7,7,80,256]{3,2,1,0:T(8,128)(2,1)}, bf16[7,7,80,256]{3,2,1,0:T(8,128)(2,1)}, u32[]{:S(2)}, u32[]{:S(2)}) collective-permute-start(bf16[7,7,80,256]{3,2,1,0:T(8,128)(2,1)} %get-tuple-element.53.hi), channel_id=1, source_target_pairs={{0,4},{4,8},{8,12},{1,5},{5,9},{9,13},{2,6},{6,10},{10,14},{3,7},{... | collective-permute-start | bytes 6021128 | tf_op jit(solution)/shard_map/ppermute | solution.py:347
  78.3 73.9 %collective-permute-start.7 = (bf16[7,7,80,256]{3,2,1,0:T(8,128)(2,1)}, bf16[7,7,80,256]{3,2,1,0:T(8,128)(2,1)}, u32[]{:S(2)}, u32[]{:S(2)}) collective-permute-start(bf16[7,7,80,256]{3,2,1,0:T(8,128)(2,1)} %get-tuple-element.49.refs_6_.lo), channel_id=1, source_target_pairs={{4,0},{8,4},{12,8},{5,1},{9,5},{13,9},{6,2},{10,6},{14,10},{7,3},{... | collective-permute-start | bytes 6021128 | tf_op jit(solution)/shard_map/ppermute | solution.py:348
  171.6 46.5 %collective-permute-start.9 = (bf16[7,24,80,256]{3,2,1,0:T(8,128)(2,1)}, bf16[7,24,80,256]{3,2,1,0:T(8,128)(2,1)}, u32[]{:S(2)}, u32[]{:S(2)}) collective-permute-start(bf16[7,24,80,256]{3,2,1,0:T(8,128)(2,1)} %tail.10.refs_4_.refs_2_.refs_5_.refs_3_.refs_6_.more_0_), channel_id=1, source_target_pairs={{0,1},{2,3},{1,0},{3,2},{4,5},{6,7},{5,4},{7,6},{8,9},{10,11},{9,8... | collective-permute-start | bytes 20643848 | tf_op jit(solution)/shard_map/ppermute | solution.py:341
  172.4 36.2 %collective-permute-start.5 = (bf16[7,10,80,256]{3,2,1,0:T(8,128)(2,1)}, bf16[7,10,80,256]{3,2,1,0:T(8,128)(2,1)}, u32[]{:S(2)}, u32[]{:S(2)}) collective-permute-start(bf16[7,10,80,256]{3,2,1,0:T(8,128)(2,1)} %get-tuple-element.48.refs_2_.more_1_), channel_id=1, source_target_pairs={{1,2},{2,1},{5,6},{6,5},{9,10},{10,9},{13,14},{14,13},{17,18},{18,... | collective-permute-start | bytes 8601608 | tf_op jit(solution)/shard_map/ppermute | solution.py:341
  175.1 57.6 %collective-permute-start.4 = (bf16[7,7,80,256]{3,2,1,0:T(8,128)(2,1)}, bf16[7,7,80,256]{3,2,1,0:T(8,128)(2,1)}, u32[]{:S(2)}, u32[]{:S(2)}) collective-permute-start(bf16[7,7,80,256]{3,2,1,0:T(8,128)(2,1)} %get-tuple-element.51.hi), channel_id=1, source_target_pairs={{0,4},{4,8},{8,12},{1,5},{5,9},{9,13},{2,6},{6,10},{10,14},{3,7},{... | collective-permute-start | bytes 6021128 | tf_op jit(solution)/shard_map/ppermute | solution.py:347
  177.9 54.8 %collective-permute-start.8 = (bf16[7,7,80,256]{3,2,1,0:T(8,128)(2,1)}, bf16[7,7,80,256]{3,2,1,0:T(8,128)(2,1)}, u32[]{:S(2)}, u32[]{:S(2)}) collective-permute-start(bf16[7,7,80,256]{3,2,1,0:T(8,128)(2,1)} %get-tuple-element.52.more_1_.lo), channel_id=1, source_target_pairs={{4,0},{8,4},{12,8},{5,1},{9,5},{13,9},{6,2},{10,6},{14,10},{7,3},{... | collective-permute-start | bytes 6021128 | tf_op jit(solution)/shard_map/ppermute | solution.py:348
  228.3 47.0 %collective-permute-start.11 = (bf16[7,7,80,256]{3,2,1,0:T(8,128)(2,1)}, bf16[7,7,80,256]{3,2,1,0:T(8,128)(2,1)}, u32[]{:S(2)}, u32[]{:S(2)}) collective-permute-start(bf16[7,7,80,256]{3,2,1,0:T(8,128)(2,1)} %get-tuple-element.57.hi), channel_id=1, source_target_pairs={{0,4},{4,8},{8,12},{1,5},{5,9},{9,13},{2,6},{6,10},{10,14},{3,7},{... | collective-permute-start | bytes 6021128 | tf_op jit(solution)/shard_map/ppermute | solution.py:347
  231.2 44.1 %collective-permute-start.12 = (bf16[7,7,80,256]{3,2,1,0:T(8,128)(2,1)}, bf16[7,7,80,256]{3,2,1,0:T(8,128)(2,1)}, u32[]{:S(2)}, u32[]{:S(2)}) collective-permute-start(bf16[7,7,80,256]{3,2,1,0:T(8,128)(2,1)} %get-tuple-element.55.more_2_.lo), channel_id=1, source_target_pairs={{4,0},{8,4},{12,8},{5,1},{9,5},{13,9},{6,2},{10,6},{14,10},{7,3},{... | collective-permute-start | bytes 6021128 | tf_op jit(solution)/shard_map/ppermute | solution.py:348
  294.8 116.7 %collective-permute-start.18 = (bf16[7,24,80,256]{3,2,1,0:T(8,128)(2,1)}, bf16[7,24,80,256]{3,2,1,0:T(8,128)(2,1)}, u32[]{:S(2)}, u32[]{:S(2)}) collective-permute-start(bf16[7,24,80,256]{3,2,1,0:T(8,128)(2,1)} %tail.12.refs_7_.refs_2_.refs_5_.refs_3_.refs_6_.refs_4_.more_0_), channel_id=1, source_target_pairs={{0,1},{2,3},{1,0},{3,2},{4,5},{6,7},{5,4},{7,6},{8,9},{10,11},{9,8... | collective-permute-start | bytes 20643848 | tf_op jit(solution)/shard_map/ppermute | solution.py:341
  294.9 48.5 %collective-permute-start.10 = (bf16[7,14,80,256]{3,2,1,0:T(8,128)(2,1)}, bf16[7,14,80,256]{3,2,1,0:T(8,128)(2,1)}, u32[]{:S(2)}, u32[]{:S(2)}) collective-permute-start(bf16[7,14,80,256]{3,2,1,0:T(8,128)(2,1)} %get-tuple-element.56.refs_1_.refs_4_.refs_7_.refs_2_.refs_5_.more_0_), channel_id=1, source_target_pairs={{1,2},{2,1},{5,6},{6,5},{9,10},{10,9},{13,14},{14,13},{17,18},{18,... | collective-permute-start | bytes 12042248 | tf_op jit(solution)/shard_map/ppermute | solution.py:341
  297.4 76.7 %collective-permute-start.14 = (bf16[7,10,80,256]{3,2,1,0:T(8,128)(2,1)}, bf16[7,10,80,256]{3,2,1,0:T(8,128)(2,1)}, u32[]{:S(2)}, u32[]{:S(2)}) collective-permute-start(bf16[7,10,80,256]{3,2,1,0:T(8,128)(2,1)} %get-tuple-element.58.refs_2_.more_1_), channel_id=1, source_target_pairs={{1,2},{2,1},{5,6},{6,5},{9,10},{10,9},{13,14},{14,13},{17,18},{18,... | collective-permute-start | bytes 8601608 | tf_op jit(solution)/shard_map/ppermute | solution.py:341
  300.4 84.6 %collective-permute-start.16 = (bf16[10,7,80,256]{3,2,1,0:T(8,128)(2,1)}, bf16[10,7,80,256]{3,2,1,0:T(8,128)(2,1)}, u32[]{:S(2)}, u32[]{:S(2)}) collective-permute-start(bf16[10,7,80,256]{3,2,1,0:T(8,128)(2,1)} %get-tuple-element.64.hi), channel_id=1, source_target_pairs={{0,4},{4,8},{8,12},{1,5},{5,9},{9,13},{2,6},{6,10},{10,14},{3,7},{... | collective-permute-start | bytes 8601608 | tf_op jit(solution)/shard_map/ppermute | solution.py:347
  305.9 79.1 %collective-permute-start.17 = (bf16[10,7,80,256]{3,2,1,0:T(8,128)(2,1)}, bf16[10,7,80,256]{3,2,1,0:T(8,128)(2,1)}, u32[]{:S(2)}, u32[]{:S(2)}) collective-permute-start(bf16[10,7,80,256]{3,2,1,0:T(8,128)(2,1)} %get-tuple-element.59.refs_6_.lo), channel_id=1, source_target_pairs={{4,0},{8,4},{12,8},{5,1},{9,5},{13,9},{6,2},{10,6},{14,10},{7,3},{... | collective-permute-start | bytes 8601608 | tf_op jit(solution)/shard_map/ppermute | solution.py:348
  353.5 68.3 %collective-permute-start.13 = (bf16[7,7,80,256]{3,2,1,0:T(8,128)(2,1)}, bf16[7,7,80,256]{3,2,1,0:T(8,128)(2,1)}, u32[]{:S(2)}, u32[]{:S(2)}) collective-permute-start(bf16[7,7,80,256]{3,2,1,0:T(8,128)(2,1)} %get-tuple-element.62.hi), channel_id=1, source_target_pairs={{0,4},{4,8},{8,12},{1,5},{5,9},{9,13},{2,6},{6,10},{10,14},{3,7},{... | collective-permute-start | bytes 6021128 | tf_op jit(solution)/shard_map/ppermute | solution.py:347
  374.1 47.6 %collective-permute-start.15 = (bf16[7,7,80,256]{3,2,1,0:T(8,128)(2,1)}, bf16[7,7,80,256]{3,2,1,0:T(8,128)(2,1)}, u32[]{:S(2)}, u32[]{:S(2)}) collective-permute-start(bf16[7,7,80,256]{3,2,1,0:T(8,128)(2,1)} %get-tuple-element.63.refs_4_.lo), channel_id=1, source_target_pairs={{4,0},{8,4},{12,8},{5,1},{9,5},{13,9},{6,2},{10,6},{14,10},{7,3},{... | collective-permute-start | bytes 6021128 | tf_op jit(solution)/shard_map/ppermute | solution.py:348
  441.3 84.4 %collective-permute-start.19 = (bf16[7,14,80,256]{3,2,1,0:T(8,128)(2,1)}, bf16[7,14,80,256]{3,2,1,0:T(8,128)(2,1)}, u32[]{:S(2)}, u32[]{:S(2)}) collective-permute-start(bf16[7,14,80,256]{3,2,1,0:T(8,128)(2,1)} %get-tuple-element.66.refs_1_.refs_4_.refs_7_.refs_2_.refs_5_.more_0_), channel_id=1, source_target_pairs={{1,2},{2,1},{5,6},{6,5},{9,10},{10,9},{13,14},{14,13},{17,18},{18,... | collective-permute-start | bytes 12042248 | tf_op jit(solution)/shard_map/ppermute | solution.py:341
  443.8 48.7 %collective-permute-start.20 = (bf16[7,7,80,256]{3,2,1,0:T(8,128)(2,1)}, bf16[7,7,80,256]{3,2,1,0:T(8,128)(2,1)}, u32[]{:S(2)}, u32[]{:S(2)}) collective-permute-start(bf16[7,7,80,256]{3,2,1,0:T(8,128)(2,1)} %get-tuple-element.67.hi), channel_id=1, source_target_pairs={{0,4},{4,8},{8,12},{1,5},{5,9},{9,13},{2,6},{6,10},{10,14},{3,7},{... | collective-permute-start | bytes 6021128 | tf_op jit(solution)/shard_map/ppermute | solution.py:347
  450.1 55.7 %collective-permute-start.21 = (bf16[7,7,80,256]{3,2,1,0:T(8,128)(2,1)}, bf16[7,7,80,256]{3,2,1,0:T(8,128)(2,1)}, u32[]{:S(2)}, u32[]{:S(2)}) collective-permute-start(bf16[7,7,80,256]{3,2,1,0:T(8,128)(2,1)} %get-tuple-element.65.more_2_.lo), channel_id=1, source_target_pairs={{4,0},{8,4},{12,8},{5,1},{9,5},{13,9},{6,2},{10,6},{14,10},{7,3},{... | collective-permute-start | bytes 6021128 | tf_op jit(solution)/shard_map/ppermute | solution.py:348
  451.3 91.8 %collective-permute-start.23 = (bf16[7,10,80,256]{3,2,1,0:T(8,128)(2,1)}, bf16[7,10,80,256]{3,2,1,0:T(8,128)(2,1)}, u32[]{:S(2)}, u32[]{:S(2)}) collective-permute-start(bf16[7,10,80,256]{3,2,1,0:T(8,128)(2,1)} %get-tuple-element.68.refs_2_.more_1_), channel_id=1, source_target_pairs={{1,2},{2,1},{5,6},{6,5},{9,10},{10,9},{13,14},{14,13},{17,18},{18,... | collective-permute-start | bytes 8601608 | tf_op jit(solution)/shard_map/ppermute | solution.py:341
  465.7 88.2 %collective-permute-start.25 = (bf16[10,7,80,256]{3,2,1,0:T(8,128)(2,1)}, bf16[10,7,80,256]{3,2,1,0:T(8,128)(2,1)}, u32[]{:S(2)}, u32[]{:S(2)}) collective-permute-start(bf16[10,7,80,256]{3,2,1,0:T(8,128)(2,1)} %get-tuple-element.74.hi), channel_id=1, source_target_pairs={{0,4},{4,8},{8,12},{1,5},{5,9},{9,13},{2,6},{6,10},{10,14},{3,7},{... | collective-permute-start | bytes 8601608 | tf_op jit(solution)/shard_map/ppermute | solution.py:347
  492.5 67.1 %collective-permute-start.26 = (bf16[10,7,80,256]{3,2,1,0:T(8,128)(2,1)}, bf16[10,7,80,256]{3,2,1,0:T(8,128)(2,1)}, u32[]{:S(2)}, u32[]{:S(2)}) collective-permute-start(bf16[10,7,80,256]{3,2,1,0:T(8,128)(2,1)} %get-tuple-element.69.refs_6_.lo), channel_id=1, source_target_pairs={{4,0},{8,4},{12,8},{5,1},{9,5},{13,9},{6,2},{10,6},{14,10},{7,3},{... | collective-permute-start | bytes 8601608 | tf_op jit(solution)/shard_map/ppermute | solution.py:348
  535.9 50.9 %collective-permute-start.22 = (bf16[7,7,80,256]{3,2,1,0:T(8,128)(2,1)}, bf16[7,7,80,256]{3,2,1,0:T(8,128)(2,1)}, u32[]{:S(2)}, u32[]{:S(2)}) collective-permute-start(bf16[7,7,80,256]{3,2,1,0:T(8,128)(2,1)} %get-tuple-element.72.hi), channel_id=1, source_target_pairs={{0,4},{4,8},{8,12},{1,5},{5,9},{9,13},{2,6},{6,10},{10,14},{3,7},{... | collective-permute-start | bytes 6021128 | tf_op jit(solution)/shard_map/ppermute | solution.py:347
  541.9 48.9 %collective-permute-start.24 = (bf16[7,7,80,256]{3,2,1,0:T(8,128)(2,1)}, bf16[7,7,80,256]{3,2,1,0:T(8,128)(2,1)}, u32[]{:S(2)}, u32[]{:S(2)}) collective-permute-start(bf16[7,7,80,256]{3,2,1,0:T(8,128)(2,1)} %get-tuple-element.73.refs_4_.lo), channel_id=1, source_target_pairs={{4,0},{8,4},{12,8},{5,1},{9,5},{13,9},{6,2},{10,6},{14,10},{7,3},{... | collective-permute-start | bytes 6021128 | tf_op jit(solution)/shard_map/ppermute | solution.py:348
